TPU v7x, 128 devices: a whole 4x4x4 slice. The times are simulated.
128 devices in a mesh: f: 16 (over z, y), h: 8 (over x, core).
Axes of the slice: x: 4, y: 4, z: 4, core: 2. Of those that a mesh axis runs over, the one named last changes fastest.
Arguments:
- x: bfloat16 [4096, 3072], P(None, 'h')
- g1: float32 [3072], P('h')
- g2: float32 [3072], P('h')
- w_gate: bfloat16 [3072, 24576], P('h', 'f')
- w_up: bfloat16 [3072, 24576], P('h', 'f')
- w_down: bfloat16 [24576, 3072], P('f', 'h')
- o: bfloat16 [4096, 4096], P(None, 'f')
- w_o: bfloat16 [4096, 3072], P('f', 'h')
- w_qkv: bfloat16 [3072, 12288], P('h', 'f')
Outputs:
- output 1: bfloat16 [4096, 3072], P(None, 'h')
- output 2: bfloat16 [4096, 12288], P(None, 'f')
All inputs are finite; a program needn't handle non-finite values.
Results may differ from a plain program's by a relative error of at most 0.0040629.
Values are sent between devices in bfloat16 or wider.
A program may use at most 1 GiB of HBM per device.

v0:
```python
import jax
import jax.numpy as jnp
from jax import lax
from jax.sharding import PartitionSpec as P

EPS = 1e-6


def _dot(a, b):
    return jnp.dot(a, b, preferred_element_type=jnp.float32)


def _norm(x, g, d):
    xf = x.astype(jnp.float32)
    ss = lax.psum(jnp.sum(xf * xf, axis=-1, keepdims=True), 'h')
    r = lax.rsqrt(ss / d + EPS)
    return (xf * r * g).astype(jnp.bfloat16)


def solution(mesh):
    h = mesh.shape['h']

    def body(x, g1, g2, w_gate, w_up, w_down, o, w_o, w_qkv):
        d = x.shape[1] * h
        n = _norm(x, g1, d)
        gt, up = lax.psum((_dot(n, w_gate), _dot(n, w_up)), 'h')
        a = (jax.nn.silu(gt) * up).astype(jnp.bfloat16)
        y = lax.psum(_dot(a, w_down) + _dot(o, w_o), 'f')
        x_next = (x.astype(jnp.float32) + y).astype(jnp.bfloat16)
        n1 = _norm(x_next, g2, d)
        qkv = lax.psum(_dot(n1, w_qkv), 'h').astype(jnp.bfloat16)
        return x_next, qkv

    in_specs = (P(None, 'h'), P('h'), P('h'), P('h', 'f'), P('h', 'f'), P('f', 'h'),
                P(None, 'f'), P('f', 'h'), P('h', 'f'))
    return jax.shard_map(body, mesh=mesh, in_specs=in_specs,
                         out_specs=(P(None, 'h'), P(None, 'f')), check_vma=False)
```

profile of v0, /device:TPU:1, one launch (start us, length us, event | category | flops | bytes accessed | tf_op | source)
XLA Modules:
  0.0 883.4 jit_solution(13729055453753115793)
XLA Ops:
  7.2 0.0 copy-start
  7.2 0.0 all-reduce.7.cloned.1.call-start
  7.2 2.7 fusion.4
  10.0 23.6 %psum.42 = f32[4096,1]{0,1:T(1,128)S(1)} all-reduce(f32[4096,1]{0,1:T(1,128)S(1)} %bitcast.14), channel_id=1, replica_groups=mesh['f'=16,'h'=8] {'h'}, use_global_device_ids=true, to_apply=%region_1.0 | all-reduce | flops 4096 | bytes 32768 | tf_op jit(solution)/shard_map/psum | solution.py:15
  33.6 0.0 copy-start.1
  33.6 0.0 copy-start.2
  33.6 0.0 copy-start.5
  33.6 13.6 %fusion.12 = f32[4096,1536]{1,0:T(8,128)} fusion(bf16[384,1536]{1,0:T(8,128)(2,1)} %param.13, bf16[4096,384]{1,0:T(8,128)(2,1)} %param.9, f32[384]{0:T(512)} %param.10, f32[4096]{0:T(1024)S(1)} %bitcast.10), kind=kOutput, calls=%fused_computation.18 | convolution fusion | flops 4838129664 | bytes 29509120 | tf_op jit(solution)/shard_map/dot_general | solution.py:10
  47.2 0.0 copy-done.1
  47.2 0.0 copy-done.2
  47.2 11.8 %fusion.14 = f32[4096,1536]{1,0:T(8,128)} fusion(bf16[384,1536]{1,0:T(8,128)(2,1)S(1)} %copy-done.2, bf16[4096,384]{1,0:T(8,128)(2,1)S(1)} %copy-done.1, f32[384]{0:T(512)S(1)} %copy-done.5, f32[4096]{0:T(1024)S(1)} %bitcast.11), kind=kOutput, calls=%fused_computation.19 | convolution fusion | flops 4838129664 | bytes 29509120 | tf_op jit(solution)/shard_map/dot_general | solution.py:10
  59.0 0.0 all-reduce.7.cloned.1.call-update
  59.1 0.0 all-reduce.5.cloned.1.call-start
  59.1 500.2 %all-reduce.7.cloned.1.call-done = (f32[4096,1536]{1,0:T(8,128)}, f32[4096,1536]{1,0:T(8,128)}) async-done(((f32[4096,1536]{1,0:T(8,128)}, f32[4096,1536]{1,0:T(8,128)}), (f32[4096,1536]{1,0:T(8,128)}, f32[4096,1536]{1,0:T(8,128)})) %all-reduce.7.cloned.1.call-update) | async-done | bytes 50331664 | tf_op jit(solution)/shard_map/psum | solution.py:26
  559.3 18.2 %fusion = f32[4096,384]{1,0:T(8,128)S(1)} fusion(bf16[1536,384]{1,0:T(8,128)(2,1)S(1)} %copy-done.7, f32[4096,1536]{1,0:T(8,128)} %get-tuple-element.2, f32[4096,1536]{1,0:T(8,128)} %get-tuple-element.3), kind=kOutput, calls=%fused_computation.1 | convolution fusion | flops 4869586944 | bytes 57802752 | tf_op jit(solution)/shard_map/dot_general | solution.py:10
  577.6 4.0 convolution_add_fusion
  581.5 0.0 all-reduce.5.cloned.1.call-update
  581.5 0.0 copy-start.3
  581.5 0.0 copy-start.6
  581.6 122.1 %all-reduce.5.cloned.1.call-done = f32[4096,384]{1,0:T(8,128)} async-done(((f32[4096,384]{1,0:T(8,128)}), f32[4096,384]{1,0:T(8,128)}) %all-reduce.5.cloned.1.call-update) | async-done | bytes 6291472 | tf_op jit(solution)/shard_map/psum | solution.py:28
  703.7 6.3 fusion.1
  710.0 22.7 %psum.46 = f32[4096,1]{0,1:T(1,128)S(1)} all-reduce(f32[4096,1]{0,1:T(1,128)S(1)} %bitcast.13), channel_id=1, replica_groups=mesh['f'=16,'h'=8] {'h'}, use_global_device_ids=true, to_apply=%region_6.7 | all-reduce | flops 4096 | bytes 32768 | tf_op jit(solution)/shard_map/psum | solution.py:15
  732.7 9.9 %fusion.8 = f32[4096,768]{1,0:T(8,128)} fusion(bf16[384,768]{1,0:T(8,128)(2,1)S(1)} %copy-done.3, bf16[4096,384]{1,0:T(8,128)(2,1)} %get-tuple-element.5, f32[384]{0:T(512)S(1)} %copy-done.6, f32[4096]{0:T(1024)S(1)} %bitcast.12), kind=kOutput, calls=%fused_computation.15 | convolution fusion | flops 2422210560 | bytes 16336384 | tf_op jit(solution)/shard_map/dot_general | solution.py:10
  742.7 133.8 %all-reduce.8 = bf16[4096,768]{1,0:T(8,128)(2,1)} all-reduce(f32[4096,768]{1,0:T(8,128)} %fusion.8), channel_id=1, replica_groups=mesh['f'=16,'h'=8] {'h'}, use_global_device_ids=true, to_apply=%region_7.8 | all-reduce | flops 3145728 | bytes 18874368 | tf_op jit(solution)/shard_map/psum | solution.py:31
  (10 shorter events, 0.1 us)
Async XLA Ops:
  7.2 570.4 %copy-start = (bf16[4096,256]{1,0:T(8,128)(2,1)S(1)}, bf16[4096,256]{1,0:T(8,128)(2,1)}, u32[]{:S(2)}) copy-start(bf16[4096,256]{1,0:T(8,128)(2,1)} %param.15) | copy-start | bytes 6291460
  7.2 552.2 %all-reduce.7.cloned.1.call-start = ((), (), s32[]{:S(2)}) async-start(), calls=%async_computation.1 | async-start | bytes 100663296 | tf_op jit(solution)/shard_map/psum | solution.py:26
  33.6 13.7 %copy-start.1 = (bf16[4096,384]{1,0:T(8,128)(2,1)S(1)}, bf16[4096,384]{1,0:T(8,128)(2,1)}, u32[]{:S(2)}) copy-start(bf16[4096,384]{1,0:T(8,128)(2,1)} %param.9) | copy-start | bytes 9437188
  33.6 13.6 %copy-start.2 = (bf16[384,1536]{1,0:T(8,128)(2,1)S(1)}, bf16[384,1536]{1,0:T(8,128)(2,1)}, u32[]{:S(2)}) copy-start(bf16[384,1536]{1,0:T(8,128)(2,1)} %param.12) | copy-start | bytes 3538948
  33.6 13.6 %copy-start.5 = (f32[384]{0:T(512)S(1)}, f32[384]{0:T(512)}, u32[]{:S(2)}) copy-start(f32[384]{0:T(512)} %param.10) | copy-start | bytes 4612
  59.0 500.3 %copy-start.7 = (bf16[1536,384]{1,0:T(8,128)(2,1)S(1)}, bf16[1536,384]{1,0:T(8,128)(2,1)}, u32[]{:S(2)}) copy-start(bf16[1536,384]{1,0:T(8,128)(2,1)} %param.14) | copy-start | bytes 3538948
  59.1 644.6 %all-reduce.5.cloned.1.call-start = ((), (), s32[]{:S(2)}) async-start(), calls=%async_computation | async-start | bytes 12582912 | tf_op jit(solution)/shard_map/psum | solution.py:28
  559.3 18.2 %copy-start.4 = (bf16[256,384]{1,0:T(8,128)(2,1)S(1)}, bf16[256,384]{1,0:T(8,128)(2,1)}, u32[]{:S(2)}) copy-start(bf16[256,384]{1,0:T(8,128)(2,1)} %param.16) | copy-start | bytes 589828
  581.5 151.2 %copy-start.3 = (bf16[384,768]{1,0:T(8,128)(2,1)S(1)}, bf16[384,768]{1,0:T(8,128)(2,1)}, u32[]{:S(2)}) copy-start(bf16[384,768]{1,0:T(8,128)(2,1)} %param.17) | copy-start | bytes 1769476
  581.5 151.2 %copy-start.6 = (f32[384]{0:T(512)S(1)}, f32[384]{0:T(512)}, u32[]{:S(2)}) copy-start(f32[384]{0:T(512)} %param.11) | copy-start | bytes 4612
Sparse Core Ops, SparseCore 0:
  59.2 500.1 all-reduce.6
  581.7 121.9 all-reduce.4
where the time goes:
time: 884 us; the launch traced here: 883 us
  waiting for transfers between devices  622 us (70%)
  blocking collectives  180 us (20%)
  matrix products  57.5 us (7%)
  between operations  14.1 us (2%)
  other arithmetic  9.11 us (1%)
    psum x1, waiting for transfers between devices, body(): gt, up = lax.psum((_dot(n, w_gate), _dot(n, w_up)), 'h')  500 us
    psum x1, blocking collectives, body(): qkv = lax.psum(_dot(n1, w_qkv), 'h').astype(jnp.bfloat16)  134 us
    psum x1, waiting for transfers between devices, body(): y = lax.psum(_dot(a, w_down) + _dot(o, w_o), 'f')  122 us
    dot_general x5, matrix products, _dot(): return jnp.dot(a, b, preferred_element_type=jnp.float32)  57.5 us
    psum x2, blocking collectives, _norm(): ss = lax.psum(jnp.sum(xf * xf, axis=-1, keepdims=True), 'h')  46.2 us
  transfers between devices with their start and end apart: 2, of which 2 were waited for; matrix products, arithmetic and copies ran while one was open for 0% of the time, Pallas kernels for 0%

commit v1 on v0

v1 whole, which is shorter than its diff:
```python
import jax
import jax.numpy as jnp
from jax import lax
from jax.sharding import PartitionSpec as P

EPS = 1e-6


def _dot(a, b):
    return jnp.dot(a, b, preferred_element_type=jnp.float32)


def _norm(xf, g):
    r = lax.rsqrt(jnp.mean(xf * xf, axis=-1, keepdims=True) + EPS)
    return (xf * r * g).astype(jnp.bfloat16)


def solution(mesh):
    nh = mesh.shape['h']
    nf = mesh.shape['f']

    def body(x, g1, g2, w_gate, w_up, w_down, o, w_o, w_qkv):
        t, dh = x.shape
        th = t // nh
        tb = th // nf
        d = dh * nh
        ih = lax.axis_index('h')
        i_f = lax.axis_index('f')

        def gather_h(w, axis):
            return lax.all_gather(w, 'h', axis=axis, tiled=True)

        xs = lax.dynamic_slice(x.reshape(nh, nf, tb, dh), (0, i_f, 0, 0), (nh, 1, tb, dh))
        xs = xs.reshape(nh, tb, dh)
        xs = lax.all_to_all(xs, 'h', split_axis=0, concat_axis=0, tiled=True)
        g = lax.all_gather(jnp.stack([g1, g2]), 'h', axis=1, tiled=True)
        xs = xs.transpose(1, 0, 2).reshape(tb, d)
        xf = xs.astype(jnp.float32)
        n = lax.all_gather(_norm(xf, g[0]), 'f', axis=0, tiled=True)
        wg = gather_h(w_gate, 0)
        wu = gather_h(w_up, 0)
        a = (jax.nn.silu(_dot(n, wg)) * _dot(n, wu)).astype(jnp.bfloat16)
        wd = gather_h(w_down, 1)
        wo = gather_h(w_o, 1)
        ot = lax.dynamic_slice(o, (ih * th, 0), (th, o.shape[1]))
        y = _dot(a, wd) + _dot(ot, wo)
        y = lax.psum_scatter(y, 'f', scatter_dimension=0, tiled=True)
        xn = (xf + y).astype(jnp.bfloat16)
        n1 = lax.all_gather(_norm(xn.astype(jnp.float32), g[1]), 'f', axis=0, tiled=True)
        xo = xn.reshape(tb, nh, dh).transpose(1, 0, 2)
        xo = lax.all_to_all(xo, 'h', split_axis=0, concat_axis=0, tiled=True)
        xo = lax.all_gather(xo, 'f', axis=0, tiled=False)
        x_next = xo.transpose(1, 0, 2, 3).reshape(t, dh)
        wqkv = gather_h(w_qkv, 0)
        qkv = _dot(n1, wqkv).astype(jnp.bfloat16)
        qkv = lax.all_gather(qkv, 'h', axis=0, tiled=True)
        return x_next, qkv

    in_specs = (P(None, 'h'), P('h'), P('h'), P('h', 'f'), P('h', 'f'), P('f', 'h'),
                P(None, 'f'), P('f', 'h'), P('h', 'f'))
    return jax.shard_map(body, mesh=mesh, in_specs=in_specs,
                         out_specs=(P(None, 'h'), P(None, 'f')), check_vma=False)
```

time: 884 us -> 551 us (0.62)
  waiting for transfers between devices: 622 us -> 442 us
  blocking collectives: 180 us -> 25.9 us
  local copies, waits for them, and re-layouts: 0.05 us -> 14 us
  matrix products: 57.5 us -> 45.1 us
    psum x2 -> x0, waiting for transfers between devices: 622 us -> none  [the longest x1 500 us: body(): gt, up = lax.psum((_dot(n, w_gate), _dot(n, w_up)), 'h')]
    all_gather x0 -> x9, waiting for transfers between devices: none -> 360 us  [the longest x5 185 us: gather_h(): return lax.all_gather(w, 'h', axis=axis, tiled=True)]
    psum x3 -> x0, blocking collectives: 180 us -> none  [the longest x1 134 us: body(): qkv = lax.psum(_dot(n1, w_qkv), 'h').astype(jnp.bfloat16)]
    reduce_scatter x0 -> x1, waiting for transfers between devices: none -> 78.8 us  [body(): y = lax.psum_scatter(y, 'f', scatter_dimension=0, tiled=True)]
    all_gather x0 -> x1, blocking collectives: none -> 13.4 us  [body(): g = lax.all_gather(jnp.stack([g1, g2]), 'h', axis=1, tiled=True)]
    all_to_all x0 -> x1, blocking collectives: none -> 12.5 us  [body(): xo = lax.all_to_all(xo, 'h', split_axis=0, concat_axis=0, tiled=True)]
    dot_general x5 -> x4, matrix products: 57.5 us -> 45.1 us  [_dot(): return jnp.dot(a, b, preferred_element_type=jnp.float32)]
  transfers between devices with their start and end apart: 2 -> 11, of which waited for: 2 -> 10; matrix products, arithmetic and copies ran while one was open for 0% -> 8% of each run, Pallas kernels for 0% -> 0%
where the time goes in v1:
time: 551 us
  waiting for transfers between devices  442 us (80%)
  matrix products  45.1 us (8%)
  blocking collectives  25.9 us (5%)
  between operations  14.2 us (3%)
  local copies, waits for them, and re-layouts  14 us (3%)
  starting transfers between devices  6.34 us (1%)
    all_gather x5, waiting for transfers between devices, gather_h(): return lax.all_gather(w, 'h', axis=axis, tiled=True)  185 us
    reduce_scatter x1, waiting for transfers between devices, body(): y = lax.psum_scatter(y, 'f', scatter_dimension=0, tiled=True)  78.8 us
    all_gather x1, waiting for transfers between devices, body(): lax.all_gather(_norm(xn.astype(jnp.float32), g[1]), 'f', axis=0, tiled=True)  48.8 us
    dot_general x4, matrix products, _dot(): return jnp.dot(a, b, preferred_element_type=jnp.float32)  45.1 us
    all_gather x1, waiting for transfers between devices, body(): n = lax.all_gather(_norm(xf, g[0]), 'f', axis=0, tiled=True)  45 us
    all_gather x1, waiting for transfers between devices, body(): xo = lax.all_gather(xo, 'f', axis=0, tiled=False)  41.9 us
    all_gather x1, waiting for transfers between devices, body(): qkv = lax.all_gather(qkv, 'h', axis=0, tiled=True)  39.3 us
    all_gather x1, blocking collectives, body(): g = lax.all_gather(jnp.stack([g1, g2]), 'h', axis=1, tiled=True)  13.4 us
  transfers between devices with their start and end apart: 11, of which 10 were waited for; matrix products, arithmetic and copies ran while one was open for 8% of the time, Pallas kernels for 0%

profile of v1, /device:TPU:1, one launch (start us, length us, event | category | flops | bytes accessed | tf_op | source)
XLA Modules:
  0.0 550.7 jit_solution(14202913162703220094)
XLA Ops:
  7.2 1.9 copy-done
  9.1 0.7 dynamic-slice_bitcast_fusion
  9.8 5.8 %all-to-all-start = ((bf16[8,32,384]{2,1,0:T(8,128)(2,1)}), bf16[8,32,384]{2,1,0:T(8,128)(2,1)S(1)}, u32[]{:S(2)}, u32[]{:S(2)}) async-start(bf16[8,32,384]{2,1,0:T(8,128)(2,1)} %dynamic-slice_bitcast_fusion), calls=%async_computation | async-start | bytes 393216 | tf_op jit(solution)/shard_map/all_to_all | solution.py:35
  16.9 13.4 %all_gather.33 = f32[2,3072]{1,0:T(2,128)S(1)} all-gather(f32[2,384]{1,0:T(2,128)S(1)} %pad_maximum_fusion), channel_id=1, replica_groups=mesh['f'=16,'h'=8] {'h'}, dimensions={1}, use_global_device_ids=true | all-gather | bytes 27648 | tf_op jit(solution)/shard_map/all_gather | solution.py:36
  30.6 0.8 multiply_convert_fusion
  34.1 45.0 %all-gather.11.cloned.1.call-done = bf16[512,3072]{1,0:T(8,128)(2,1)} async-done(((bf16[32,3072]{1,0:T(8,128)(2,1)}), bf16[512,3072]{1,0:T(8,128)(2,1)}) %all-gather.11.cloned.1.call-update) | async-done | bytes 3145744 | tf_op jit(solution)/shard_map/all_gather | solution.py:39
  79.1 56.2 %all-gather.13.cloned.1.call-done = bf16[3072,1536]{1,0:T(8,128)(2,1)} async-done(((bf16[384,1536]{1,0:T(8,128)(2,1)}), bf16[3072,1536]{1,0:T(8,128)(2,1)}) %all-gather.13.cloned.1.call-update) | async-done | bytes 9437200 | tf_op jit(solution)/shard_map/all_gather | solution.py:31
  135.3 10.5 %fusion.10 = f32[512,1536]{1,0:T(8,128)} fusion(bf16[512,3072]{1,0:T(8,128)(2,1)} %all-gather.11.cloned.1.call-done, bf16[3072,1536]{1,0:T(8,128)(2,1)} %all-gather.13.cloned.1.call-done), kind=kOutput, calls=%fused_computation.24 | convolution fusion | flops 4831838208 | bytes 15728640 | tf_op jit(solution)/shard_map/dot_general | solution.py:10
  145.9 45.4 %all-gather.15.cloned.1.call-done = bf16[3072,1536]{1,0:T(8,128)(2,1)} async-done(((bf16[384,1536]{1,0:T(8,128)(2,1)}), bf16[3072,1536]{1,0:T(8,128)(2,1)}) %all-gather.15.cloned.1.call-update) | async-done | bytes 9437200 | tf_op jit(solution)/shard_map/all_gather | solution.py:31
  191.3 55.7 %all-gather.17.cloned.1.call-done = bf16[1536,3072]{1,0:T(8,128)(2,1)} async-done(((bf16[1536,384]{1,0:T(8,128)(2,1)}), bf16[1536,3072]{1,0:T(8,128)(2,1)}) %all-gather.17.cloned.1.call-update) | async-done | bytes 9437200 | tf_op jit(solution)/shard_map/all_gather | solution.py:31
  247.0 20.8 %fusion.1 = f32[512,3072]{1,0:T(8,128)} fusion(bf16[1536,3072]{1,0:T(8,128)(2,1)} %all-gather.17.cloned.1.call-done, bf16[512,3072]{1,0:T(8,128)(2,1)} %all-gather.11.cloned.1.call-done, bf16[3072,1536]{1,0:T(8,128)(2,1)} %all-gather.15.cloned.1.call-done, f32[512,1536]{1,0:T(8,128)} %fusion.10), kind=kOutput, calls=%fused_computation.4 | convolution fusion | flops 9668395008 | bytes 31457280 | tf_op jit(solution)/shard_map/dot_general | solution.py:10
  267.8 5.5 all-gather.19.cloned.1.call-done
  273.2 7.0 %convolution_add_fusion = f32[512,3072]{1,0:T(8,128)} fusion(f32[512,3072]{1,0:T(8,128)} %fusion.1, bf16[256,3072]{1,0:T(8,128)(2,1)} %all-gather.19.cloned.1.call-done, bf16[4096,256]{1,0:T(8,128)(2,1)} %param.15, s32[]{:T(128)S(6)} %select_n.7), kind=kOutput, calls=%fused_computation | convolution fusion | flops 806879232 | bytes 14417924 | tf_op jit(solution)/shard_map/dot_general | solution.py:10
  281.1 78.8 %reduce-scatter.2.cloned.1.call-done = f32[32,3072]{1,0:T(8,128)} async-done(((f32[512,3072]{1,0:T(8,128)}), f32[32,3072]{1,0:T(8,128)}) %reduce-scatter.2.cloned.1.call-update) | async-done | bytes 393232 | tf_op jit(solution)/shard_map/reduce_scatter | solution.py:47
  359.9 1.1 fusion.2
  361.0 0.8 fusion.4
  361.9 12.5 %all_to_all.10 = bf16[8,32,384]{2,1,0:T(8,128)(2,1)} all-to-all(bf16[8,32,384]{2,1,0:T(8,128)(2,1)S(1)} %bitcast.36), channel_id=1, replica_groups=mesh['f'=16,'h'=8] {'h'}, dimensions={0} | all-to-all | bytes 393216 | tf_op jit(solution)/shard_map/all_to_all | solution.py:51
  374.7 22.3 %all-gather.23.cloned.1.call-done = bf16[3072,768]{1,0:T(8,128)(2,1)} async-done(((bf16[384,768]{1,0:T(8,128)(2,1)}), bf16[3072,768]{1,0:T(8,128)(2,1)}) %all-gather.23.cloned.1.call-update) | async-done | bytes 4718608 | tf_op jit(solution)/shard_map/all_gather | solution.py:31
  397.1 48.8 %all-gather.21.cloned.1.call-done = bf16[512,3072]{1,0:T(8,128)(2,1)} async-done(((bf16[32,3072]{1,0:T(8,128)(2,1)}), bf16[512,3072]{1,0:T(8,128)(2,1)}) %all-gather.21.cloned.1.call-update) | async-done | bytes 3145744 | tf_op jit(solution)/shard_map/all_gather | solution.py:49
  445.9 6.8 %convolution_convert_fusion = bf16[512,768]{1,0:T(8,128)(2,1)} fusion(bf16[512,3072]{1,0:T(8,128)(2,1)} %all-gather.21.cloned.1.call-done, bf16[3072,768]{1,0:T(8,128)(2,1)} %all-gather.23.cloned.1.call-done), kind=kOutput, calls=%fused_computation.3 | convolution fusion | flops 2416312320 | bytes 8650752 | tf_op jit(solution)/shard_map/dot_general | solution.py:10
  452.6 41.9 %all-gather.27.cloned.1.call-done = bf16[128,32,384]{2,1,0:T(8,128)(2,1)} async-done(((bf16[8,32,384]{2,1,0:T(8,128)(2,1)}), bf16[128,32,384]{2,1,0:T(8,128)(2,1)}) %all-gather.27.cloned.1.call-update) | async-done | bytes 3145744 | tf_op jit(solution)/shard_map/all_gather | solution.py:52
  494.5 4.0 copy.20
  498.5 39.3 %all-gather.25.cloned.1.call-done = bf16[4096,768]{1,0:T(8,128)(2,1)} async-done(((bf16[512,768]{1,0:T(8,128)(2,1)}), bf16[4096,768]{1,0:T(8,128)(2,1)}) %all-gather.25.cloned.1.call-update) | async-done | bytes 6291472 | tf_op jit(solution)/shard_map/all_gather | solution.py:56
  537.8 6.0 %copy.27 = bf16[4096,768]{1,0:T(8,128)(2,1)} copy(bf16[4096,768]{1,0:T(8,128)(2,1)} %all-gather.25.cloned.1.call-done) | data formatting | bytes 12582912
  (34 shorter events, 5.4 us)
Async XLA Ops:
  7.2 1.9 copy-start
  9.8 20.6 %all-to-all-start = ((bf16[8,32,384]{2,1,0:T(8,128)(2,1)}), bf16[8,32,384]{2,1,0:T(8,128)(2,1)S(1)}, u32[]{:S(2)}, u32[]{:S(2)}) async-start(bf16[8,32,384]{2,1,0:T(8,128)(2,1)} %dynamic-slice_bitcast_fusion), calls=%async_computation | async-start | bytes 393216 | tf_op jit(solution)/shard_map/all_to_all | solution.py:35
  15.6 63.6 %all-gather.11.cloned.1.call-start = ((), (), s32[]{:S(2)}) async-start(), calls=%async_computation.3 | async-start | bytes 3342336 | tf_op jit(solution)/shard_map/all_gather | solution.py:39
  31.4 103.9 %all-gather.13.cloned.1.call-start = ((), (), s32[]{:S(2)}) async-start(), calls=%async_computation.4 | async-start | bytes 10616832 | tf_op jit(solution)/shard_map/all_gather | solution.py:31
  32.2 159.1 %all-gather.15.cloned.1.call-start = ((), (), s32[]{:S(2)}) async-start(), calls=%async_computation.5 | async-start | bytes 10616832 | tf_op jit(solution)/shard_map/all_gather | solution.py:31
  32.9 214.1 %all-gather.17.cloned.1.call-start = ((), (), s32[]{:S(2)}) async-start(), calls=%async_computation.6 | async-start | bytes 10616832 | tf_op jit(solution)/shard_map/all_gather | solution.py:31
  33.5 239.8 %all-gather.19.cloned.1.call-start = ((), (), s32[]{:S(2)}) async-start(), calls=%async_computation.7 | async-start | bytes 1769472 | tf_op jit(solution)/shard_map/all_gather | solution.py:31
  34.1 325.8 %reduce-scatter.2.cloned.1.call-start = ((), (), s32[]{:S(2)}) async-start(), calls=%async_computation.8 | async-start | bytes 6684672 | tf_op jit(solution)/shard_map/reduce_scatter | solution.py:47
  280.3 116.7 %all-gather.23.cloned.1.call-start = ((), (), s32[]{:S(2)}) async-start(), calls=%async_computation.10 | async-start | bytes 5308416 | tf_op jit(solution)/shard_map/all_gather | solution.py:31
  281.1 164.8 %all-gather.21.cloned.1.call-start = ((), (), s32[]{:S(2)}) async-start(), calls=%async_computation.9 | async-start | bytes 3342336 | tf_op jit(solution)/shard_map/all_gather | solution.py:49
  361.9 132.7 %all-gather.27.cloned.1.call-start = ((), (), s32[]{:S(2)}) async-start(), calls=%async_computation.12 | async-start | bytes 3342336 | tf_op jit(solution)/shard_map/all_gather | solution.py:52
  374.5 163.3 %all-gather.25.cloned.1.call-start = ((), (), s32[]{:S(2)}) async-start(), calls=%async_computation.11 | async-start | bytes 7077888 | tf_op jit(solution)/shard_map/all_gather | solution.py:56
  537.8 6.0 %copy-start.1 = (bf16[4096,384]{1,0:T(8,128)(2,1)S(1)}, bf16[4096,384]{1,0:T(8,128)(2,1)}, u32[]{:S(2)}) copy-start(bf16[4096,384]{1,0:T(8,128)(2,1)} %param.9) | copy-start | bytes 9437188
Sparse Core Ops, SparseCore 0:
  31.5 47.5 all-gather.10
  80.8 54.4 all-gather.12
  137.0 54.2 all-gather.14
  192.8 54.0 all-gather.16
  248.5 24.6 all-gather.18
  280.4 79.3 reduce-scatter.1
  361.6 35.4 all-gather.22
  399.8 46.0 all-gather.20
  448.0 46.4 all-gather.26
  496.6 41.1 all-gather.24

commit v2 on v0

v2 whole, which is shorter than its diff:
```python
import functools

import jax
import jax.numpy as jnp
from jax import lax
from jax.experimental import pallas as pl
from jax.experimental.pallas import tpu as pltpu
from jax.sharding import PartitionSpec as P

EPS = 1e-6
MESH = pl.DeviceIdType.MESH
ANY = pl.BlockSpec(memory_space=pl.ANY)
VM = pl.BlockSpec(memory_space=pltpu.VMEM)
BF = jnp.bfloat16
F32 = jnp.float32


def _dot(a, b):
    return jnp.dot(a, b, preferred_element_type=jnp.float32)


class Pos:
    def __init__(self):
        self.f = lax.axis_index('f')
        self.h = lax.axis_index('h')
        self.z, self.y = self.f // 4, self.f % 4
        self.x, self.c = self.h // 2, self.h % 2
        self.j = self.x // 2
        self.q = quarter(self.h)
        ax = self.x + 1 - 2 * (self.x % 2)
        self.A = (self.f, 2 * ax + self.c)
        self.B = (self.f, 2 * (3 - self.x) + self.c)
        self.C = (self.f, self.h + 1 - 2 * self.c)
        self.AC = (self.f, 2 * ax + 1 - self.c)

    def H(self, d):
        return (self.f, (self.h + d) % 8)

    def Y(self, d):
        return (4 * self.z + (self.y + d) % 4, self.h)

    def Z(self, d):
        return (4 * ((self.z + d) % 4) + self.y, self.h)


def quarter(h):
    x = h // 2
    return 2 * ((x + x // 2) % 2) + h % 2


class Comm:
    def __init__(self, ssem, rsem, lsem):
        self.ssem, self.rsem, self.lsem = ssem, rsem, lsem
        self.k = 0
        self.lk = 0
        self.sent = []

    def send(self, src, dst, dev):
        c = pltpu.make_async_remote_copy(src_ref=src, dst_ref=dst, send_sem=self.ssem.at[self.k],
                                         recv_sem=self.rsem.at[self.k], device_id=dev, device_id_type=MESH)
        self.k += 1
        c.start()
        self.sent.append(c)
        return c

    def local(self, src, dst):
        c = pltpu.make_async_copy(src, dst, self.lsem.at[self.lk])
        self.lk += 1
        c.start()
        return c

    def finish(self):
        for c in self.sent:
            c.wait_send()


def barrier(devs):
    b = pltpu.get_barrier_semaphore()
    for d in devs:
        pl.semaphore_signal(b, inc=1, device_id=d, device_id_type=MESH)
    pl.semaphore_wait(b, len(devs))


def run(*gens):
    live = []
    for g in gens:
        t = next(g, None)
        if t is not None:
            live.append([t, g])
    while live:
        e = min(live, key=lambda v: v[0])
        t = next(e[1], None)
        if t is None:
            live.remove(e)
        else:
            e[0] = t


def ring_ag(cm, own, blk, half, m, plus, minus, t0, u):
    lo, hi = (m + 3) % 4, (m + 1) % 4
    p0 = cm.send(own, blk(m), plus)
    m0 = cm.send(own, blk(m), minus)
    yield t0 + u
    p0.wait_recv()
    p1 = cm.send(half(lo, 0), half(lo, 0), plus)
    m0.wait_recv()
    m1 = cm.send(half(hi, 1), half(hi, 1), minus)
    yield t0 + 1.5 * u
    p1.wait_recv()
    m1.wait_recv()


def k1(x, g, wg, wu, n_o, wg_o, wu_o, xs_o, g_o, xs, gb, nb, wst, ssem, rsem, lsem):
    p = Pos()
    cm = Comm(ssem, rsem, lsem)
    barrier([p.H(d) for d in range(1, 8)] + [p.Y(1), p.Y(-1), p.Z(1), p.Z(-1)])
    tb = xs.shape[1]
    ww = wst.shape[2]

    def rows(q):
        return x.at[pl.ds(pl.multiple_of(1024 * q + tb * p.f, tb), tb), :]

    xin = []
    for d in range(1, 8):
        t = p.H(d)
        xin.append(cm.send(rows(quarter(t[1])), xs.at[p.h], t))
        xin.append(cm.send(g, gb.at[p.h], t))
    loc = [cm.local(rows(p.q), xs.at[p.h]), cm.local(g, gb.at[p.h])]

    def cols(w, j):
        return w.at[:, pl.ds(pl.multiple_of(ww * j, ww), ww)]

    def weights():
        ws = ((wg, wg_o), (wu, wu_o))
        stage = [cm.local(cols(w, p.j), wst.at[k]) for k, (w, _) in enumerate(ws)]
        b, a, c = [], [], []
        for w, wo in ws:
            b.append(cm.send(cols(w, 1 - p.j), wo.at[p.h], p.B))
            a.append(cm.send(cols(w, p.j), wo.at[p.h], p.A))
            c.append(cm.send(cols(w, p.j), wo.at[p.h], p.C))
        yield 8.0
        out = []
        for k, (w, wo) in enumerate(ws):
            stage[k].wait()
            out.append(cm.local(wst.at[k], wo.at[p.h]))
        a2 = []
        for k, (w, wo) in enumerate(ws):
            yield 14.0 + 12.5 * k
            b[k].wait_recv()
            s = wo.at[p.B[1]]
            a2.append(cm.send(s, s, p.A))
            c.append(cm.send(s, s, p.C))
            a[k].wait_recv()
            s = wo.at[p.A[1]]
            c.append(cm.send(s, s, p.C))
        for k, (w, wo) in enumerate(ws):
            yield 40.0 + 12.5 * k
            a2[k].wait_recv()
            s = wo.at[(2 * (3 - p.A[1] // 2)) + p.c]
            c.append(cm.send(s, s, p.C))
        yield 55.0
        for v in c:
            v.wait_recv()
        for v in out:
            v.wait()

    def tokens():
        yield 5.0
        for v in xin:
            v.wait_recv()
        for v in loc:
            v.wait()
        ss = jnp.zeros((tb, 1), F32)
        for k in range(8):
            v = xs[k].astype(F32)
            ss = ss + jnp.sum(v * v, axis=-1, keepdims=True)
        r = lax.rsqrt(ss / 3072.0 + EPS)
        dh = xs.shape[2]
        for k in range(8):
            nb[:, dh * k:dh * (k + 1)] = (xs[k].astype(F32) * r * gb[k, 0:1, :]).astype(BF)
        xs_o[...] = xs[...]
        g_o[...] = gb[...]
        yield from plane_ag(cm, p, nb, n_o, 10.0, 4.0, 17.0)

    run(tokens(), weights())
    cm.finish()


def plane_ag(cm, p, nb, n_o, t0, u1, u2):
    hb = nb.shape[0] // 2
    w = nb.shape[1] // 2
    ca, cb = pl.ds(0, w), pl.ds(w, w)
    own = cm.local(nb, n_o.at[p.z, p.y])

    def first():
        ya = ring_ag(cm, nb.at[:, ca], lambda i: n_o.at[p.z, i, :, ca],
                     lambda i, s: n_o.at[p.z, i, pl.ds(hb * s, hb), ca], p.y, p.Y(1), p.Y(-1), t0, u1)
        zb = ring_ag(cm, nb.at[:, cb], lambda i: n_o.at[i, p.y, :, cb],
                     lambda i, s: n_o.at[i, p.y, pl.ds(hb * s, hb), cb], p.z, p.Z(1), p.Z(-1), t0, u1)
        for t, _ in zip(ya, zb):
            yield t
        list(zb)

    yield from first()
    own.wait()
    t1 = t0 + 1.5 * u1

    def second():
        za = ring_ag(cm, n_o.at[p.z, :, :, ca], lambda i: n_o.at[i, :, :, ca],
                     lambda i, s: n_o.at[i, pl.ds(2 * s, 2), :, ca], p.z, p.Z(1), p.Z(-1), t1, u2)
        yb = ring_ag(cm, n_o.at[:, p.y, :, cb], lambda i: n_o.at[:, i, :, cb],
                     lambda i, s: n_o.at[pl.ds(2 * s, 2), i, :, cb], p.y, p.Y(1), p.Y(-1), t1, u2)
        for t, _ in zip(za, yb):
            yield t
        list(yb)

    yield from second()


def k2(a, wd, wo, a_o, wd_o, wo_o, dst, ost, ssem, rsem, lsem):
    p = Pos()
    cm = Comm(ssem, rsem, lsem)
    barrier([p.A, p.B, p.C])
    w = wd.shape[1]

    def slot(o, h):
        return o.at[:, pl.ds(pl.multiple_of(w * (h % 4), w), w)]

    ra = cm.send(a, a_o, p.B)
    st = [cm.local(wd, dst), cm.local(wo, ost)]
    fa = [cm.send(wd, slot(wd_o, p.h), p.A), cm.send(wo, slot(wo_o, p.h), p.A)]
    c = [cm.send(wd, slot(wd_o, p.h), p.C), cm.send(wo, slot(wo_o, p.h), p.C)]
    out = []
    for v, s, o in zip(st, (dst, ost), (wd_o, wo_o)):
        v.wait()
        out.append(cm.local(s, slot(o, p.h)))
    for v, o in zip(fa, (wd_o, wo_o)):
        v.wait_recv()
        s = slot(o, p.A[1])
        c.append(cm.send(s, s, p.C))
    for v in c:
        v.wait_recv()
    for v in out:
        v.wait()
    ra.wait_recv()
    cm.finish()


def ring_rs(cm, get, r1p, r1m, ap, am, fp, fm, res, m, plus, minus, t0, u):
    lo, hi, far = (m + 3) % 4, (m + 1) % 4, (m + 2) % 4
    hb = r1p.shape[-2]
    f0, f1 = (Ellipsis, pl.ds(0, hb), slice(None)), (Ellipsis, pl.ds(hb, hb), slice(None))
    p0 = cm.send(get(far, 0), r1p, plus)
    m0 = cm.send(get(far, 1), r1m, minus)
    p1 = cm.send(get(hi, 1), fp.at[f1], plus)
    m1 = cm.send(get(lo, 0), fm.at[f0], minus)
    yield t0 + 0.5 * u
    p0.wait_recv()
    ap[...] = r1p[...] + get(hi, 0)[...]
    p2 = cm.send(ap, fp.at[f0], plus)
    m0.wait_recv()
    am[...] = r1m[...] + get(lo, 1)[...]
    m2 = cm.send(am, fm.at[f1], minus)
    yield t0 + u
    p1.wait_recv()
    m1.wait_recv()
    yield t0 + 1.5 * u
    p2.wait_recv()
    m2.wait_recv()
    res[f0] = (fp[f0] + fm[f0]) + get(m, 0)[...]
    res[f1] = (fp[f1] + fm[f1]) + get(m, 1)[...]


def k3(y, xs, g, wq, xn_o, n_o, wq_o,
       r1, a1, f1, s1, r2, a2, f2, s2, xr, nbuf, wst, ssem, rsem, lsem):
    p = Pos()
    cm = Comm(ssem, rsem, lsem)
    barrier([p.Y(1), p.Y(-1), p.Z(1), p.Z(-1), p.H(2), p.H(-2), p.B, p.C])
    tb = y.shape[2]
    hb = tb // 2
    w = y.shape[3] // 2
    ca, cb = pl.ds(0, w), pl.ds(w, w)

    def weights():
        st = cm.local(wq, wst)
        c = [cm.send(wq, wq_o.at[p.h], p.C)]

        def blk(i):
            return wq_o.at[2 * i + p.c]

        hr = wq.shape[0] // 2

        def half(i, s):
            return wq_o.at[2 * i + p.c, pl.ds(hr * s, hr), :]

        m = p.x
        lo, hi, far = (m + 3) % 4, (m + 1) % 4, (m + 2) % 4
        p0 = cm.send(wq, blk(m), p.H(2))
        m0 = cm.send(wq, blk(m), p.H(-2))
        yield 1.0
        st.wait()
        own = cm.local(wst, wq_o.at[p.h])
        yield 16.0
        p0.wait_recv()
        p1 = cm.send(half(lo, 0), half(lo, 0), p.H(2))
        c.append(cm.send(blk(lo), blk(lo), p.C))
        m0.wait_recv()
        m1 = cm.send(half(hi, 1), half(hi, 1), p.H(-2))
        c.append(cm.send(blk(hi), blk(hi), p.C))
        yield 28.0
        p1.wait_recv()
        m1.wait_recv()
        c.append(cm.send(blk(far), blk(far), p.C))
        yield 34.0
        own.wait()
        for v in c:
            v.wait_recv()

    def tokens():
        ga = ring_rs(cm, lambda i, s: y.at[:, i, pl.ds(hb * s, hb), ca], r1.at[0], r1.at[1], a1.at[0], a1.at[1],
                     f1.at[0], f1.at[1], s1.at[0], p.y, p.Y(1), p.Y(-1), 0.0, 17.0)
        gb = ring_rs(cm, lambda i, s: y.at[i, :, pl.ds(hb * s, hb), cb], r1.at[2], r1.at[3], a1.at[2], a1.at[3],
                     f1.at[2], f1.at[3], s1.at[1], p.z, p.Z(1), p.Z(-1), 0.0, 17.0)
        for t, _ in zip(ga, gb):
            yield t
        list(gb)
        ga = ring_rs(cm, lambda i, s: s1.at[0, i, pl.ds(hb * s, hb), :], r2.at[0], r2.at[1], a2.at[0], a2.at[1],
                     f2.at[0], f2.at[1], s2.at[0], p.z, p.Z(1), p.Z(-1), 26.0, 6.0)
        gb = ring_rs(cm, lambda i, s: s1.at[1, i, pl.ds(hb * s, hb), :], r2.at[2], r2.at[3], a2.at[2], a2.at[3],
                     f2.at[2], f2.at[3], s2.at[1], p.y, p.Y(1), p.Y(-1), 26.0, 6.0)
        for t, _ in zip(ga, gb):
            yield t
        list(gb)
        dh = xs.shape[2]
        for k in range(4):
            yk = s2[k // 2, :, dh * (k % 2):dh * (k % 2 + 1)]
            xn_o[:, dh * k:dh * (k + 1)] = (xs[4 * p.j + k].astype(F32) + yk).astype(BF)
        ex = cm.send(xn_o.at[pl.ds(pl.multiple_of(hb * (1 - p.j), hb), hb), :], xr, p.B)
        mine = xn_o[pl.ds(pl.multiple_of(hb * p.j, hb), hb), :].astype(F32)
        ss = jnp.sum(mine * mine, axis=-1, keepdims=True)
        yield 36.0
        ex.wait_recv()
        oth = xr[...].astype(F32)
        ss = ss + jnp.sum(oth * oth, axis=-1, keepdims=True)
        r = lax.rsqrt(ss / 3072.0 + EPS)
        for k in range(4):
            cs = slice(dh * k, dh * (k + 1))
            nbuf[p.j, :, cs] = (mine[:, cs] * r * g[4 * p.j + k, 1:2, :]).astype(BF)
            nbuf[1 - p.j, :, cs] = (oth[:, cs] * r * g[4 * (1 - p.j) + k, 1:2, :]).astype(BF)
        yield from plane_ag2(cm, p, nbuf, n_o, 38.0, 2.0, 8.5)

    run(tokens(), weights())
    cm.finish()


def plane_ag2(cm, p, nb, n_o, t0, u1, u2):
    hb = nb.shape[1] // 2
    w = nb.shape[2]
    ca, cb = pl.ds(0, w), pl.ds(w, w)
    own = [cm.local(nb.at[0], n_o.at[p.z, p.y, :, ca]), cm.local(nb.at[1], n_o.at[p.z, p.y, :, cb])]
    ya = ring_ag(cm, nb.at[0], lambda i: n_o.at[p.z, i, :, ca],
                 lambda i, s: n_o.at[p.z, i, pl.ds(hb * s, hb), ca], p.y, p.Y(1), p.Y(-1), t0, u1)
    zb = ring_ag(cm, nb.at[1], lambda i: n_o.at[i, p.y, :, cb],
                 lambda i, s: n_o.at[i, p.y, pl.ds(hb * s, hb), cb], p.z, p.Z(1), p.Z(-1), t0, u1)
    for t, _ in zip(ya, zb):
        yield t
    list(zb)
    for v in own:
        v.wait()
    t1 = t0 + 1.5 * u1
    za = ring_ag(cm, n_o.at[p.z, :, :, ca], lambda i: n_o.at[i, :, :, ca],
                 lambda i, s: n_o.at[i, pl.ds(2 * s, 2), :, ca], p.z, p.Z(1), p.Z(-1), t1, u2)
    yb = ring_ag(cm, n_o.at[:, p.y, :, cb], lambda i: n_o.at[:, i, :, cb],
                 lambda i, s: n_o.at[pl.ds(2 * s, 2), i, :, cb], p.y, p.Y(1), p.Y(-1), t1, u2)
    for t, _ in zip(za, yb):
        yield t
    list(yb)


def k5(qkv, xn, q_o, x_o, xq, ssem, rsem, lsem):
    p = Pos()
    cm = Comm(ssem, rsem, lsem)
    barrier([p.Y(1), p.Y(-1), p.Z(1), p.Z(-1), p.H(2), p.H(-2), p.A, p.C, p.AC])
    dh = xq.shape[2]

    def cols(h):
        return xn.at[:, pl.ds(pl.multiple_of(dh * (h % 4), dh), dh)]

    ex = [cm.send(cols(d[1]), xq.at[p.q], d) for d in (p.A, p.C, p.AC)]
    lo = cm.local(cols(p.h), xq.at[p.q])

    def proj():
        def blk(x, c):
            h = 2 * x + c
            return q_o.at[quarter(h), :, h // 4]

        def half(x, c, s):
            h = 2 * x + c
            return q_o.at[quarter(h), pl.ds(8 * s, 8), h // 4]

        m = p.x
        l, r, far = (m + 3) % 4, (m + 1) % 4, (m + 2) % 4
        own = cm.local(qkv, blk(m, p.c))
        p0 = cm.send(qkv, blk(m, p.c), p.H(2))
        m0 = cm.send(qkv, blk(m, p.c), p.H(-2))
        c = [cm.send(qkv, blk(m, p.c), p.C)]
        yield 17.5
        p0.wait_recv()
        s = half(l, p.c, 0)
        p1 = cm.send(s, s, p.H(2))
        m0.wait_recv()
        s = half(r, p.c, 1)
        m1 = cm.send(s, s, p.H(-2))
        for b in (blk(l, p.c), blk(r, p.c)):
            c.append(cm.send(b, b, p.C))
        yield 28.0
        p1.wait_recv()
        s = half(far, p.c, 0)
        c.append(cm.send(s, s, p.C))
        m1.wait_recv()
        s = half(far, p.c, 1)
        c.append(cm.send(s, s, p.C))
        own.wait()
        for v in c:
            v.wait_recv()

    def resid():
        yield 3.0
        for v in ex:
            v.wait_recv()
        lo.wait()
        qa, qb = pl.ds(0, 2), pl.ds(2, 2)
        own = cm.local(xq, x_o.at[:, p.z, p.y])
        ya = ring_ag(cm, xq.at[qa], lambda i: x_o.at[qa, p.z, i],
                     lambda i, s: x_o.at[s, p.z, i], p.y, p.Y(1), p.Y(-1), 3.5, 2.0)
        zb = ring_ag(cm, xq.at[qb], lambda i: x_o.at[qb, i, p.y],
                     lambda i, s: x_o.at[2 + s, i, p.y], p.z, p.Z(1), p.Z(-1), 3.5, 2.0)
        for t, _ in zip(ya, zb):
            yield t
        list(zb)
        own.wait()
        za = ring_ag(cm, x_o.at[qa, p.z], lambda i: x_o.at[qa, i],
                     lambda i, s: x_o.at[s, i], p.z, p.Z(1), p.Z(-1), 7.0, 8.5)
        yb = ring_ag(cm, x_o.at[qb, :, p.y], lambda i: x_o.at[qb, :, i],
                     lambda i, s: x_o.at[2 + s, :, i], p.y, p.Y(1), p.Y(-1), 7.0, 8.5)
        for t, _ in zip(za, yb):
            yield t
        list(yb)

    run(resid(), proj())
    cm.finish()


def _call(body, cid, out, out_specs, in_specs, scratch, args, nsem=64, nl=8):
    return pl.pallas_call(
        body,
        out_shape=[jax.ShapeDtypeStruct(s, d) for s, d in out],
        in_specs=in_specs,
        out_specs=out_specs,
        scratch_shapes=scratch + [pltpu.SemaphoreType.DMA((nsem,)), pltpu.SemaphoreType.DMA((nsem,)),
                                  pltpu.SemaphoreType.DMA((nl,))],
        compiler_params=pltpu.CompilerParams(collective_id=cid, has_side_effects=True,
                                             vmem_limit_bytes=48 * 1024 * 1024),
        name=body.__name__,
    )(*args)


def solution(mesh):
    def body(x, g1, g2, w_gate, w_up, w_down, o, w_o, w_qkv):
        t, dh = x.shape
        d = dh * 8
        ff = w_gate.shape[1]
        tq = t // 4
        tb = tq // 16
        h = lax.axis_index('h')
        q = quarter(h)
        j = h // 4
        g = jnp.concatenate([jnp.stack([g1, g2]), jnp.zeros((6, dh), F32)], axis=0)
        fh = ff // 2
        n, wg, wu, xs, gf = _call(
            k1, 1,
            [((4, 4, tb, d), BF), ((8, dh, fh), BF), ((8, dh, fh), BF), ((8, tb, dh), BF), ((8, 8, dh), F32)],
            [ANY, ANY, ANY, VM, VM], [ANY] * 4,
            [pltpu.VMEM((8, tb, dh), BF), pltpu.VMEM((8, 8, dh), F32), pltpu.VMEM((tb, d), BF),
             pltpu.VMEM((2, dh, fh), BF)],
            (x, g, w_gate, w_up))
        n = n.reshape(tq, d)
        gt = _dot(n, wg.reshape(d, fh))
        up = _dot(n, wu.reshape(d, fh))
        a = (jax.nn.silu(gt) * up).astype(BF)
        a2, wd, wo = _call(
            k2, 2, [((tq, fh), BF), ((ff, d // 2), BF), ((w_o.shape[0], d // 2), BF)],
            [ANY] * 3, [ANY] * 3,
            [pltpu.VMEM(w_down.shape, BF), pltpu.VMEM(w_o.shape, BF)],
            (a, w_down, w_o))
        ot = lax.dynamic_slice(o, (q * tq, 0), (tq, o.shape[1]))
        wd0 = lax.dynamic_slice(wd, (j * fh, 0), (fh, d // 2))
        wd1 = lax.dynamic_slice(wd, ((1 - j) * fh, 0), (fh, d // 2))
        y = _dot(a, wd0) + _dot(a2, wd1) + _dot(ot, wo)
        w2 = d // 4
        hb = tb // 2
        xn, n1, wq = _call(
            k3, 3,
            [((tb, d // 2), BF), ((4, 4, hb, d), BF), ((8, dh, w_qkv.shape[1]), BF)],
            [VM, ANY, ANY], [VM, VM, VM, ANY],
            [pltpu.VMEM((4, 4, hb, w2), F32), pltpu.VMEM((4, 4, hb, w2), F32), pltpu.VMEM((4, 4, tb, w2), F32),
             pltpu.VMEM((2, 4, tb, w2), F32),
             pltpu.VMEM((4, hb, w2), F32), pltpu.VMEM((4, hb, w2), F32), pltpu.VMEM((4, tb, w2), F32),
             pltpu.VMEM((2, tb, w2), F32),
             pltpu.VMEM((hb, d // 2), BF), pltpu.VMEM((2, hb, d // 2), BF), pltpu.VMEM(w_qkv.shape, BF)],
            (y.reshape(4, 4, tb, d // 2), xs, gf, w_qkv))
        qkv = _dot(n1.reshape(tq // 2, d), wq.reshape(d, -1)).astype(BF)
        qo, xo = _call(
            k5, 4,
            [((4, 16, 2, hb, qkv.shape[1]), BF), ((4, 4, 4, tb, dh), BF)],
            [ANY, ANY], [VM, VM],
            [pltpu.VMEM((4, tb, dh), BF)],
            (qkv.reshape(16, hb, -1), xn))
        return xo.reshape(t, dh), qo.reshape(t, -1)

    in_specs = (P(None, 'h'), P('h'), P('h'), P('h', 'f'), P('h', 'f'), P('f', 'h'),
                P(None, 'f'), P('f', 'h'), P('h', 'f'))
    return jax.shard_map(body, mesh=mesh, in_specs=in_specs,
                         out_specs=(P(None, 'h'), P(None, 'f')), check_vma=False)
```

time: 884 us -> 260 us (0.29)
  waiting for transfers between devices: 622 us -> 0 us
  Pallas kernels: 0 us -> 216 us
  blocking collectives: 180 us -> 0 us
  matrix products: 57.5 us -> 29.7 us
  between operations: 14.1 us -> 0.9 us
  local copies, waits for them, and re-layouts: 0.05 us -> 12.6 us
  other arithmetic: 9.11 us -> 0.07 us
    psum x2 -> x0, waiting for transfers between devices: 622 us -> none  [the longest x1 500 us: body(): gt, up = lax.psum((_dot(n, w_gate), _dot(n, w_up)), 'h')]
    pallas_call x0 -> x4, Pallas kernels: none -> 216 us  [_call(): pl.pallas_call(body, out_shape=[jax.ShapeDtypeStruct(s, d) for s, d in ou...]
    psum x3 -> x0, blocking collectives: 180 us -> none  [the longest x1 134 us: body(): qkv = lax.psum(_dot(n1, w_qkv), 'h').astype(jnp.bfloat16)]
    dot_general x5 -> x6, matrix products: 57.5 us -> 29.7 us  [_dot(): return jnp.dot(a, b, preferred_element_type=jnp.float32)]
    unnamed x16 -> x24, local copies, waits for them, and re-layouts: 0.05 us -> 11.1 us
    reduce_sum x2 -> x0, other arithmetic: 9.05 us -> none  [_norm(): ss = lax.psum(jnp.sum(xf * xf, axis=-1, keepdims=True), 'h')]
  transfers between devices with their start and end apart: 2 -> 0, of which waited for: 2 -> 0; matrix products, arithmetic and copies ran while one was open for 0% -> 0% of each run, Pallas kernels for 0% -> 0%
where the time goes in v2:
time: 260 us; the launch traced here: 259 us
  Pallas kernels  216 us (83%)
  matrix products  29.7 us (11%)
  local copies, waits for them, and re-layouts  12.6 us (5%)
    pallas_call x4, Pallas kernels, _call(): pl.pallas_call(body, out_shape=[jax.ShapeDtypeStruct(s, d) for s, d in ou...  216 us
    dot_general x6, matrix products, _dot(): return jnp.dot(a, b, preferred_element_type=jnp.float32)  29.7 us
    unnamed x24, local copies, waits for them, and re-layouts  11.1 us

profile of v2, /device:TPU:1, one launch (start us, length us, event | category | flops | bytes accessed | tf_op | source)
XLA Modules:
  0.0 259.5 jit_solution(8945161978871106300)
XLA Ops:
  0.6 0.0 copy-start
  0.7 0.1 pad.2.clone
  0.8 0.8 stack.6
  1.6 0.7 stack.7
  2.3 0.1 maximum_maximum_fusion.g
  2.4 1.9 copy-done.1
  4.3 1.3 copy-done.2
  5.5 1.3 copy-done.3
  6.8 66.0 %k1.1 = (bf16[4,4,64,3072]{3,2,1,0:T(8,128)(2,1)}, bf16[8,384,768]{2,1,0:T(8,128)(2,1)}, bf16[8,384,768]{2,1,0:T(8,128)(2,1)}, bf16[8,64,384]{2,1,0:T(8,128)(2,1)S(1)}, f32[8,8,384]{2,1,0:T(8,128)S(1)}) custom-call(bf16[4096,384]{1,0:T(8,128)(2,1)S(1)} %copy-done.1, f32[8,384]{1,0:T(8,128)S(1)} %maximum_maximum_fusion.g, bf16[384,1536]{1,0:T(8,128)(2,1)S(1)} %copy-done.2, ...), custom_call_target="tpu_custom_call" | custom-call | tf_op jit(solution)/shard_map/k1/pallas_call | solution.py:455
  72.8 8.7 %fusion.8 = f32[1024,768]{1,0:T(8,128)S(1)} fusion(bf16[1024,3072]{1,0:T(8,128)(2,1)} %bitcast.23, bf16[3072,768]{1,0:T(8,128)(2,1)} %bitcast.26), kind=kOutput, calls=%fused_computation.12 | convolution fusion | flops 4831838208 | bytes 14155776 | tf_op jit(solution)/shard_map/dot_general | solution.py:19
  81.5 0.0 copy-start.4
  81.5 0.0 copy-start.6
  81.5 5.3 %multiply_convert_fusion.a = bf16[1024,768]{1,0:T(8,128)(2,1)S(1)} fusion(f32[1024,768]{1,0:T(8,128)S(1)} %fusion.8, bf16[1024,3072]{1,0:T(8,128)(2,1)S(1)} %bitcast.24, bf16[3072,768]{1,0:T(8,128)(2,1)S(1)} %bitcast.25), kind=kOutput, calls=%fused_computation.1 | convolution fusion | flops 4836556800 | bytes 15728640 | tf_op jit(solution)/shard_map/dot_general | solution.py:19
  86.9 38.4 %k2.1 = (bf16[1024,768]{1,0:T(8,128)(2,1)S(1)}, bf16[1536,1536]{1,0:T(8,128)(2,1)}, bf16[256,1536]{1,0:T(8,128)(2,1)S(1)}) custom-call(bf16[1024,768]{1,0:T(8,128)(2,1)S(1)} %multiply_convert_fusion.a, bf16[1536,384]{1,0:T(8,128)(2,1)S(1)} %copy-done.4, bf16[256,384]{1,0:T(8,128)(2,1)S(1)} %copy-done.6), custom_call_target="tpu_custom_call" | custom-call | tf_op jit(solution)/shard_map/k2/pallas_call | solution.py:455
  125.2 4.4 %fusion = f32[1024,1536]{1,0:T(8,128)S(1)} fusion(bf16[1024,768]{1,0:T(8,128)(2,1)S(1)} %get-tuple-element.19, bf16[1536,1536]{1,0:T(8,128)(2,1)} %get-tuple-element.18, s32[]{:T(128)S(6)} %select_n.32), kind=kOutput, calls=%fused_computation.2 | convolution fusion | flops 2415919104 | bytes 10223620 | tf_op jit(solution)/shard_map/dot_general | solution.py:19
  129.7 2.6 %fusion.2 = f32[1024,1536]{1,0:T(8,128)S(1)} fusion(bf16[1024,768]{1,0:T(8,128)(2,1)S(1)} %multiply_convert_fusion.a, bf16[1536,1536]{1,0:T(8,128)(2,1)S(1)} %copy-done.10, s32[]{:T(128)S(6)} %select_n.31), kind=kOutput, calls=%fused_computation.4 | convolution fusion | flops 2415919104 | bytes 10223620 | tf_op jit(solution)/shard_map/dot_general | solution.py:19
  132.3 0.0 copy-start.5
  132.3 3.8 %add_add_fusion = f32[1024,1536]{1,0:T(8,128)} fusion(f32[1024,1536]{1,0:T(8,128)S(1)} %fusion.2, f32[1024,1536]{1,0:T(8,128)S(1)} %fusion, bf16[256,1536]{1,0:T(8,128)(2,1)S(1)} %get-tuple-element.20, bf16[4096,256]{1,0:T(8,128)(2,1)S(1)} %copy-done, s32[]{:T(128)S(6)} %select_n.37), kind=kOutput, calls=%fused_computation | convolution fusion | flops 808452096 | bytes 20185092 | tf_op jit(solution)/shard_map/dot_general | solution.py:19
  136.1 66.4 %k3.1 = (bf16[64,1536]{1,0:T(8,128)(2,1)S(1)}, bf16[4,4,32,3072]{3,2,1,0:T(8,128)(2,1)S(1)}, bf16[8,384,768]{2,1,0:T(8,128)(2,1)}) custom-call(f32[4,4,64,1536]{3,2,1,0:T(8,128)} %bitcast.21, bf16[8,64,384]{2,1,0:T(8,128)(2,1)S(1)} %get-tuple-element.21.xs, f32[8,8,384]{2,1,0:T(8,128)S(1)} %get-tuple-element.22.g, bf16[384,768]{1,0:T(8,128)(2,1)S(1)} %copy-done.5), custom_call_target="tpu_custom_call" | custom-call | tf_op jit(solution)/shard_map/k3/pallas_call | solution.py:455
  202.5 4.9 %convolution_convert_fusion = bf16[512,768]{1,0:T(8,128)(2,1)S(1)} fusion(bf16[512,3072]{1,0:T(8,128)(2,1)S(1)} %bitcast.20, bf16[3072,768]{1,0:T(8,128)(2,1)} %bitcast.27), kind=kOutput, calls=%fused_computation.6 | convolution fusion | flops 2416312320 | bytes 8650752 | tf_op jit(solution)/shard_map/dot_general | solution.py:19
  207.4 45.4 %k5.1 = (bf16[4,16,2,32,768]{4,3,2,1,0:T(8,128)(2,1)}, bf16[4,4,4,64,384]{4,3,2,1,0:T(8,128)(2,1)S(1)}) custom-call(bf16[16,32,768]{2,1,0:T(8,128)(2,1)S(1)} %bitcast.19, bf16[64,1536]{1,0:T(8,128)(2,1)S(1)} %get-tuple-element.25.xn), custom_call_target="tpu_custom_call" | custom-call | tf_op jit(solution)/shard_map/k5/pallas_call | solution.py:455
  252.9 1.7 copy.13
  254.5 2.2 copy-done.7
  256.8 2.7 %copy.14 = bf16[4096,768]{1,0:T(8,128)(2,1)} copy(bf16[4096,768]{1,0:T(8,128)(2,1)S(1)} %bitcast.22) | data formatting | bytes 12582912
  (15 shorter events, 0.0 us)
Async XLA Ops:
  0.6 131.7 %copy-start = (bf16[4096,256]{1,0:T(8,128)(2,1)S(1)}, bf16[4096,256]{1,0:T(8,128)(2,1)}, u32[]{:S(2)}) copy-start(bf16[4096,256]{1,0:T(8,128)(2,1)} %param.15) | copy-start | bytes 6291460
  2.4 1.9 copy-start.1
  4.3 1.3 copy-start.2
  5.5 1.3 copy-start.3
  72.8 8.7 %copy-start.8 = (bf16[4,4,64,3072]{3,2,1,0:T(8,128)(2,1)S(1)}, bf16[4,4,64,3072]{3,2,1,0:T(8,128)(2,1)}, u32[]{:S(2)}) copy-start(bf16[4,4,64,3072]{3,2,1,0:T(8,128)(2,1)} %get-tuple-element.15) | copy-start | bytes 18874372
  72.8 8.7 %copy-start.9 = (bf16[8,384,768]{2,1,0:T(8,128)(2,1)S(1)}, bf16[8,384,768]{2,1,0:T(8,128)(2,1)}, u32[]{:S(2)}) copy-start(bf16[8,384,768]{2,1,0:T(8,128)(2,1)} %get-tuple-element.17) | copy-start | bytes 14155780
  81.5 5.3 %copy-start.4 = (bf16[1536,384]{1,0:T(8,128)(2,1)S(1)}, bf16[1536,384]{1,0:T(8,128)(2,1)}, u32[]{:S(2)}) copy-start(bf16[1536,384]{1,0:T(8,128)(2,1)} %wd.1) | copy-start | bytes 3538948
  81.5 5.3 %copy-start.6 = (bf16[256,384]{1,0:T(8,128)(2,1)S(1)}, bf16[256,384]{1,0:T(8,128)(2,1)}, u32[]{:S(2)}) copy-start(bf16[256,384]{1,0:T(8,128)(2,1)} %wo.1) | copy-start | bytes 589828
  125.2 4.4 %copy-start.10 = (bf16[1536,1536]{1,0:T(8,128)(2,1)S(1)}, bf16[1536,1536]{1,0:T(8,128)(2,1)}, u32[]{:S(2)}) copy-start(bf16[1536,1536]{1,0:T(8,128)(2,1)} %get-tuple-element.18) | copy-start | bytes 14155780
  132.3 3.8 %copy-start.5 = (bf16[384,768]{1,0:T(8,128)(2,1)S(1)}, bf16[384,768]{1,0:T(8,128)(2,1)}, u32[]{:S(2)}) copy-start(bf16[384,768]{1,0:T(8,128)(2,1)} %wq.1) | copy-start | bytes 1769476
  252.8 3.9 %copy-start.7 = (bf16[4,16,2,32,768]{4,3,2,1,0:T(8,128)(2,1)S(1)}, bf16[4,16,2,32,768]{4,3,2,1,0:T(8,128)(2,1)}, u32[]{:S(2)}) copy-start(bf16[4,16,2,32,768]{4,3,2,1,0:T(8,128)(2,1)} %get-tuple-element.27) | copy-start | bytes 18874372

commit v3 on v2

--- a/solution.py
+++ b/solution.py
@@ -11,6 +11,7 @@
 MESH = pl.DeviceIdType.MESH
 ANY = pl.BlockSpec(memory_space=pl.ANY)
 VM = pl.BlockSpec(memory_space=pltpu.VMEM)
+HB = pl.BlockSpec(memory_space=pltpu.HBM)
 BF = jnp.bfloat16
 F32 = jnp.float32
 
@@ -110,12 +111,14 @@
     m1.wait_recv()
 
 
-def k1(x, g, wg, wu, n_o, wg_o, wu_o, xs_o, g_o, xs, gb, nb, wst, ssem, rsem, lsem):
+def mlp(x, g, wg, wu, wd, o, wo, y_o, xs_o, g_o,
+        xs, gb, nb, n, wgb, wub, wdb, wob, ov, a1, a2, ssem, rsem, lsem):
     p = Pos()
     cm = Comm(ssem, rsem, lsem)
     barrier([p.H(d) for d in range(1, 8)] + [p.Y(1), p.Y(-1), p.Z(1), p.Z(-1)])
-    tb = xs.shape[1]
-    ww = wst.shape[2]
+    tb, dh = xs.shape[1:]
+    ww = wgb.shape[2]
+    hb = tb // 2
 
     def rows(q):
         return x.at[pl.ds(pl.multiple_of(1024 * q + tb * p.f, tb), tb), :]
@@ -130,38 +133,44 @@
     def cols(w, j):
         return w.at[:, pl.ds(pl.multiple_of(ww * j, ww), ww)]
 
+    def slot(b, h):
+        return b.at[:, pl.ds(pl.multiple_of(dh * (h % 4), dh), dh)]
+
+    late = []
+    down_in = []
+
     def weights():
-        ws = ((wg, wg_o), (wu, wu_o))
-        stage = [cm.local(cols(w, p.j), wst.at[k]) for k, (w, _) in enumerate(ws)]
-        b, a, c = [], [], []
-        for w, wo in ws:
-            b.append(cm.send(cols(w, 1 - p.j), wo.at[p.h], p.B))
-            a.append(cm.send(cols(w, p.j), wo.at[p.h], p.A))
-            c.append(cm.send(cols(w, p.j), wo.at[p.h], p.C))
-        yield 8.0
-        out = []
-        for k, (w, wo) in enumerate(ws):
-            stage[k].wait()
-            out.append(cm.local(wst.at[k], wo.at[p.h]))
-        a2 = []
-        for k, (w, wo) in enumerate(ws):
+        ws = ((wg, wgb), (wu, wub))
+        own, b, a, c, a2_ = [], [], [], [], []
+        for w, wb in ws:
+            b.append(cm.send(cols(w, 1 - p.j), wb.at[p.h], p.B))
+            a.append(cm.send(cols(w, p.j), wb.at[p.h], p.A))
+            c.append(cm.send(cols(w, p.j), wb.at[p.h], p.C))
+            own.append(cm.local(cols(w, p.j), wb.at[p.h]))
+        own.append(cm.local(o.at[pl.ds(pl.multiple_of(1024 * p.q, 1024), 1024), :], ov))
+        for w, wb in ((wd, wdb), (wo, wob)):
+            own.append(cm.local(w, slot(wb, p.h)))
+        for k, (w, wb) in enumerate(ws):
             yield 14.0 + 12.5 * k
             b[k].wait_recv()
-            s = wo.at[p.B[1]]
-            a2.append(cm.send(s, s, p.A))
+            s = wb.at[p.B[1]]
+            a2_.append(cm.send(s, s, p.A))
             c.append(cm.send(s, s, p.C))
             a[k].wait_recv()
-            s = wo.at[p.A[1]]
+            s = wb.at[p.A[1]]
             c.append(cm.send(s, s, p.C))
-        for k, (w, wo) in enumerate(ws):
+        for w, wb in ((wd, wdb), (wo, wob)):
+            down_in.append(cm.send(w, slot(wb, p.h), p.A))
+            late.append(cm.send(w, slot(wb, p.h), p.C))
+        for k, (w, wb) in enumerate(ws):
             yield 40.0 + 12.5 * k
-            a2[k].wait_recv()
-            s = wo.at[(2 * (3 - p.A[1] // 2)) + p.c]
+            a2_[k].wait_recv()
+            s = wb.at[(2 * (3 - p.A[1] // 2)) + p.c]
             c.append(cm.send(s, s, p.C))
         yield 55.0
         for v in c:
             v.wait_recv()
-        for v in out:
+        for v in own:
             v.wait()
 
     def tokens():
@@ -175,14 +184,52 @@
             v = xs[k].astype(F32)
             ss = ss + jnp.sum(v * v, axis=-1, keepdims=True)
         r = lax.rsqrt(ss / 3072.0 + EPS)
-        dh = xs.shape[2]
         for k in range(8):
             nb[:, dh * k:dh * (k + 1)] = (xs[k].astype(F32) * r * gb[k, 0:1, :]).astype(BF)
         xs_o[...] = xs[...]
         g_o[...] = gb[...]
-        yield from plane_ag(cm, p, nb, n_o, 10.0, 4.0, 17.0)
+        yield from plane_ag(cm, p, nb, n, 10.0, 4.0, 17.0)
 
     run(tokens(), weights())
+
+    tn = 256
+    d = n.shape[3]
+    got = []
+    for b in range(4):
+        s, zh = b // 2, b % 2
+
+        def gate_up(t, carry, b=b, s=s, zh=zh):
+            v = n[2 * zh:2 * zh + 2, :, hb * s:hb * (s + 1), :].reshape(8 * hb, d)
+            cs = pl.ds(pl.multiple_of(t * tn, tn), tn)
+            gt = _dot(v, wgb[:, :, cs].reshape(d, tn))
+            up = _dot(v, wub[:, :, cs].reshape(d, tn))
+            a1[b, :, cs] = (jax.nn.silu(gt) * up).astype(BF)
+            return carry
+
+        lax.fori_loop(0, ww // tn, gate_up, 0)
+        got.append(cm.send(a1.at[b], a2.at[b], p.B))
+
+    for v, wb in zip(down_in, (wdb, wob)):
+        v.wait_recv()
+        s = slot(wb, p.A[1])
+        late.append(cm.send(s, s, p.C))
+    for v in late:
+        v.wait_recv()
+    kn = 512
+    for b in range(4):
+        s, zh = b // 2, b % 2
+        got[b].wait_recv()
+
+        def down(t, carry, b=b, s=s, zh=zh):
+            cs = pl.ds(pl.multiple_of(t * kn, kn), kn)
+            ob = ov[512 * zh:512 * (zh + 1), :].reshape(8, tb, -1)[:, hb * s:hb * (s + 1), :].reshape(8 * hb, -1)
+            v = (_dot(a1[b], wdb[pl.ds(pl.multiple_of(ww * p.j, ww), ww), cs])
+                 + _dot(a2[b], wdb[pl.ds(pl.multiple_of(ww * (1 - p.j), ww), ww), cs])
+                 + _dot(ob, wob[:, cs]))
+            y_o[2 * zh:2 * zh + 2, :, hb * s:hb * (s + 1), cs] = v.reshape(2, 4, hb, kn)
+            return carry
+
+        lax.fori_loop(0, wdb.shape[1] // kn, down, 0)
     cm.finish()
 
 
@@ -215,35 +262,6 @@
         list(yb)
 
     yield from second()
-
-
-def k2(a, wd, wo, a_o, wd_o, wo_o, dst, ost, ssem, rsem, lsem):
-    p = Pos()
-    cm = Comm(ssem, rsem, lsem)
-    barrier([p.A, p.B, p.C])
-    w = wd.shape[1]
-
-    def slot(o, h):
-        return o.at[:, pl.ds(pl.multiple_of(w * (h % 4), w), w)]
-
-    ra = cm.send(a, a_o, p.B)
-    st = [cm.local(wd, dst), cm.local(wo, ost)]
-    fa = [cm.send(wd, slot(wd_o, p.h), p.A), cm.send(wo, slot(wo_o, p.h), p.A)]
-    c = [cm.send(wd, slot(wd_o, p.h), p.C), cm.send(wo, slot(wo_o, p.h), p.C)]
-    out = []
-    for v, s, o in zip(st, (dst, ost), (wd_o, wo_o)):
-        v.wait()
-        out.append(cm.local(s, slot(o, p.h)))
-    for v, o in zip(fa, (wd_o, wo_o)):
-        v.wait_recv()
-        s = slot(o, p.A[1])
-        c.append(cm.send(s, s, p.C))
-    for v in c:
-        v.wait_recv()
-    for v in out:
-        v.wait()
-    ra.wait_recv()
-    cm.finish()
 
 
 def ring_rs(cm, get, r1p, r1m, ap, am, fp, fm, res, m, plus, minus, t0, u):
@@ -451,7 +469,7 @@
     cm.finish()
 
 
-def _call(body, cid, out, out_specs, in_specs, scratch, args, nsem=64, nl=8):
+def _call(body, cid, out, out_specs, in_specs, scratch, args, nsem=64, nl=12):
     return pl.pallas_call(
         body,
         out_shape=[jax.ShapeDtypeStruct(s, d) for s, d in out],
@@ -460,7 +478,7 @@
         scratch_shapes=scratch + [pltpu.SemaphoreType.DMA((nsem,)), pltpu.SemaphoreType.DMA((nsem,)),
                                   pltpu.SemaphoreType.DMA((nl,))],
         compiler_params=pltpu.CompilerParams(collective_id=cid, has_side_effects=True,
-                                             vmem_limit_bytes=48 * 1024 * 1024),
+                                             vmem_limit_bytes=56 * 1024 * 1024),
         name=body.__name__,
     )(*args)
 
@@ -472,43 +490,28 @@
         ff = w_gate.shape[1]
         tq = t // 4
         tb = tq // 16
-        h = lax.axis_index('h')
-        q = quarter(h)
-        j = h // 4
         g = jnp.concatenate([jnp.stack([g1, g2]), jnp.zeros((6, dh), F32)], axis=0)
         fh = ff // 2
-        n, wg, wu, xs, gf = _call(
-            k1, 1,
-            [((4, 4, tb, d), BF), ((8, dh, fh), BF), ((8, dh, fh), BF), ((8, tb, dh), BF), ((8, 8, dh), F32)],
-            [ANY, ANY, ANY, VM, VM], [ANY] * 4,
-            [pltpu.VMEM((8, tb, dh), BF), pltpu.VMEM((8, 8, dh), F32), pltpu.VMEM((tb, d), BF),
-             pltpu.VMEM((2, dh, fh), BF)],
-            (x, g, w_gate, w_up))
-        n = n.reshape(tq, d)
-        gt = _dot(n, wg.reshape(d, fh))
-        up = _dot(n, wu.reshape(d, fh))
-        a = (jax.nn.silu(gt) * up).astype(BF)
-        a2, wd, wo = _call(
-            k2, 2, [((tq, fh), BF), ((ff, d // 2), BF), ((w_o.shape[0], d // 2), BF)],
-            [ANY] * 3, [ANY] * 3,
-            [pltpu.VMEM(w_down.shape, BF), pltpu.VMEM(w_o.shape, BF)],
-            (a, w_down, w_o))
-        ot = lax.dynamic_slice(o, (q * tq, 0), (tq, o.shape[1]))
-        wd0 = lax.dynamic_slice(wd, (j * fh, 0), (fh, d // 2))
-        wd1 = lax.dynamic_slice(wd, ((1 - j) * fh, 0), (fh, d // 2))
-        y = _dot(a, wd0) + _dot(a2, wd1) + _dot(ot, wo)
+        bf, f32 = (lambda *v: pltpu.VMEM(v, BF)), (lambda *v: pltpu.VMEM(v, F32))
+        y, xs, gf = _call(
+            mlp, 1,
+            [((4, 4, tb, d // 2), F32), ((8, tb, dh), BF), ((8, 8, dh), F32)],
+            [VM, VM, VM], [HB] * 7,
+            [bf(8, tb, dh), f32(8, 8, dh), bf(tb, d), bf(4, 4, tb, d), bf(8, dh, fh), bf(8, dh, fh),
+             bf(ff, d // 2), bf(w_o.shape[0], d // 2), bf(tq, w_o.shape[0]), bf(4, tq // 4, fh), bf(4, tq // 4, fh)],
+            (x, g, w_gate, w_up, w_down, o, w_o))
         w2 = d // 4
         hb = tb // 2
         xn, n1, wq = _call(
             k3, 3,
             [((tb, d // 2), BF), ((4, 4, hb, d), BF), ((8, dh, w_qkv.shape[1]), BF)],
-            [VM, ANY, ANY], [VM, VM, VM, ANY],
+            [VM, ANY, ANY], [VM, VM, VM, HB],
             [pltpu.VMEM((4, 4, hb, w2), F32), pltpu.VMEM((4, 4, hb, w2), F32), pltpu.VMEM((4, 4, tb, w2), F32),
              pltpu.VMEM((2, 4, tb, w2), F32),
              pltpu.VMEM((4, hb, w2), F32), pltpu.VMEM((4, hb, w2), F32), pltpu.VMEM((4, tb, w2), F32),
              pltpu.VMEM((2, tb, w2), F32),
              pltpu.VMEM((hb, d // 2), BF), pltpu.VMEM((2, hb, d // 2), BF), pltpu.VMEM(w_qkv.shape, BF)],
-            (y.reshape(4, 4, tb, d // 2), xs, gf, w_qkv))
+            (y, xs, gf, w_qkv))
         qkv = _dot(n1.reshape(tq // 2, d), wq.reshape(d, -1)).astype(BF)
         qo, xo = _call(
             k5, 4,

time: 260 us -> 241 us (0.927)
  matrix products: 29.7 us -> 6.77 us
  Pallas kernels: 216 us -> 224 us
  local copies, waits for them, and re-layouts: 12.6 us -> 8.82 us
    dot_general x6 -> x1, matrix products: 29.7 us -> 6.77 us  [_dot(): return jnp.dot(a, b, preferred_element_type=jnp.float32)]
    pallas_call x4 -> x3, Pallas kernels: 216 us -> 224 us  [_call(): pl.pallas_call(body, out_shape=[jax.ShapeDtypeStruct(s, d) for s, d in ou...]
    unnamed x24 -> x4, local copies, waits for them, and re-layouts: 11.1 us -> 7.37 us
where the time goes in v3:
time: 241 us
  Pallas kernels  224 us (93%)
  local copies, waits for them, and re-layouts  8.82 us (4%)
  matrix products  6.77 us (3%)
    pallas_call x3, Pallas kernels, _call(): pl.pallas_call(body, out_shape=[jax.ShapeDtypeStruct(s, d) for s, d in ou...  224 us
    unnamed x4, local copies, waits for them, and re-layouts  7.37 us
    dot_general x1, matrix products, _dot(): return jnp.dot(a, b, preferred_element_type=jnp.float32)  6.77 us

profile of v3, /device:TPU:1, one launch (start us, length us, event | category | flops | bytes accessed | tf_op | source)
XLA Modules:
  0.0 240.7 jit_solution(103157112633788533)
XLA Ops:
  0.6 0.1 pad.2.clone
  0.7 0.7 stack.6
  1.4 0.7 stack.7
  2.1 0.7 maximum_maximum_fusion.g
  2.8 110.1 %mlp.1 = (f32[4,4,64,1536]{3,2,1,0:T(8,128)}, bf16[8,64,384]{2,1,0:T(8,128)(2,1)}, f32[8,8,384]{2,1,0:T(8,128)}) custom-call(bf16[4096,384]{1,0:T(8,128)(2,1)} %x.1, f32[8,384]{1,0:T(8,128)} %maximum_maximum_fusion.g, bf16[384,1536]{1,0:T(8,128)(2,1)} %wg.1, bf16[384,1536]{1,0:T(8,128)(2,1)} %wu.1, bf16[1536,384]{1,0:T(8,128)(2,1)} %wd.1, ...), custom_call_target="tpu_custom_call" | custom-call | tf_op jit(solution)/shard_map/mlp/pallas_call | solution.py:473
  112.9 67.5 %k3.1 = (bf16[64,1536]{1,0:T(8,128)(2,1)}, bf16[4,4,32,3072]{3,2,1,0:T(8,128)(2,1)}, bf16[8,384,768]{2,1,0:T(8,128)(2,1)}) custom-call(f32[4,4,64,1536]{3,2,1,0:T(8,128)} %get-tuple-element.10.y, bf16[8,64,384]{2,1,0:T(8,128)(2,1)} %get-tuple-element.11.xs, f32[8,8,384]{2,1,0:T(8,128)} %get-tuple-element.12.g, bf16[384,768]{1,0:T(8,128)(2,1)} %wq.1), custom_call_target="tpu_custom_call" | custom-call | tf_op jit(solution)/shard_map/k3/pallas_call | solution.py:473
  180.4 6.8 %convolution_convert_fusion = bf16[512,768]{1,0:T(8,128)(2,1)} fusion(bf16[512,3072]{1,0:T(8,128)(2,1)} %bitcast.11, bf16[3072,768]{1,0:T(8,128)(2,1)} %bitcast.10), kind=kOutput, calls=%fused_computation | convolution fusion | flops 2416312320 | bytes 8650752 | tf_op jit(solution)/shard_map/dot_general | solution.py:20
  187.2 46.1 %k5.1 = (bf16[4,16,2,32,768]{4,3,2,1,0:T(8,128)(2,1)}, bf16[4,4,4,64,384]{4,3,2,1,0:T(8,128)(2,1)}) custom-call(bf16[16,32,768]{2,1,0:T(8,128)(2,1)} %bitcast.9, bf16[64,1536]{1,0:T(8,128)(2,1)} %get-tuple-element.15.xn), custom_call_target="tpu_custom_call" | custom-call | tf_op jit(solution)/shard_map/k5/pallas_call | solution.py:473
  233.3 0.0 copy-start
  233.3 4.0 %copy.13 = bf16[4096,384]{1,0:T(8,128)(2,1)} copy(bf16[4096,384]{1,0:T(8,128)(2,1)} %bitcast.8) | data formatting | bytes 6291456
  237.3 0.7 copy-done
  238.0 2.7 %copy.14 = bf16[4096,768]{1,0:T(8,128)(2,1)} copy(bf16[4096,768]{1,0:T(8,128)(2,1)S(1)} %bitcast.7) | data formatting | bytes 12582912
  (1 shorter events, 0.0 us)
Async XLA Ops:
  233.3 4.7 %copy-start = (bf16[4,16,2,32,768]{4,3,2,1,0:T(8,128)(2,1)S(1)}, bf16[4,16,2,32,768]{4,3,2,1,0:T(8,128)(2,1)}, u32[]{:S(2)}) copy-start(bf16[4,16,2,32,768]{4,3,2,1,0:T(8,128)(2,1)} %get-tuple-element.17) | copy-start | bytes 18874372

commit v4 on v0

v4 whole, which is shorter than its diff:
```python
import functools

import jax
import jax.numpy as jnp
from jax import lax
from jax.experimental import pallas as pl
from jax.experimental.pallas import tpu as pltpu
from jax.sharding import PartitionSpec as P

EPS = 1e-6
MESH = pl.DeviceIdType.MESH
ANY = pl.BlockSpec(memory_space=pl.ANY)
VM = pl.BlockSpec(memory_space=pltpu.VMEM)
HB = pl.BlockSpec(memory_space=pltpu.HBM)
BF = jnp.bfloat16
F32 = jnp.float32


def _dot(a, b):
    return jnp.dot(a, b, preferred_element_type=jnp.float32)


class Pos:
    def __init__(self):
        self.f = lax.axis_index('f')
        self.h = lax.axis_index('h')
        self.z, self.y = self.f // 4, self.f % 4
        self.x, self.c = self.h // 2, self.h % 2
        self.j = self.x // 2
        self.q = quarter(self.h)
        ax = self.x + 1 - 2 * (self.x % 2)
        self.A = (self.f, 2 * ax + self.c)
        self.B = (self.f, 2 * (3 - self.x) + self.c)
        self.C = (self.f, self.h + 1 - 2 * self.c)
        self.AC = (self.f, 2 * ax + 1 - self.c)

    def H(self, d):
        return (self.f, (self.h + d) % 8)

    def Y(self, d):
        return (4 * self.z + (self.y + d) % 4, self.h)

    def Z(self, d):
        return (4 * ((self.z + d) % 4) + self.y, self.h)


def quarter(h):
    x = h // 2
    return 2 * ((x + x // 2) % 2) + h % 2


class Comm:
    def __init__(self, ssem, rsem, lsem):
        self.ssem, self.rsem, self.lsem = ssem, rsem, lsem
        self.k = 0
        self.lk = 0
        self.sent = []

    def send(self, src, dst, dev):
        c = pltpu.make_async_remote_copy(src_ref=src, dst_ref=dst, send_sem=self.ssem.at[self.k],
                                         recv_sem=self.rsem.at[self.k], device_id=dev, device_id_type=MESH)
        self.k += 1
        c.start()
        self.sent.append(c)
        return c

    def local(self, src, dst):
        c = pltpu.make_async_copy(src, dst, self.lsem.at[self.lk])
        self.lk += 1
        c.start()
        return c

    def finish(self):
        for c in self.sent:
            c.wait_send()


def barrier(devs):
    b = pltpu.get_barrier_semaphore()
    for d in devs:
        pl.semaphore_signal(b, inc=1, device_id=d, device_id_type=MESH)
    pl.semaphore_wait(b, len(devs))


def run(*gens):
    live = []
    for g in gens:
        t = next(g, None)
        if t is not None:
            live.append([t, g])
    while live:
        e = min(live, key=lambda v: v[0])
        t = next(e[1], None)
        if t is None:
            live.remove(e)
        else:
            e[0] = t


def ring_ag(cm, own, blk, half, m, plus, minus, t0, u):
    lo, hi = (m + 3) % 4, (m + 1) % 4
    p0 = cm.send(own, blk(m), plus)
    m0 = cm.send(own, blk(m), minus)
    yield t0 + u
    p0.wait_recv()
    p1 = cm.send(half(lo, 0), half(lo, 0), plus)
    m0.wait_recv()
    m1 = cm.send(half(hi, 1), half(hi, 1), minus)
    yield t0 + 1.5 * u
    p1.wait_recv()
    m1.wait_recv()


def plane_ag(cm, p, own, n_o, half, t0, u1, u2):
    ya = ring_ag(cm, own(0), lambda i: n_o(p.z, i, 0), lambda i, s: half(n_o(p.z, i, 0), s), p.y, p.Y(1), p.Y(-1), t0, u1)
    zb = ring_ag(cm, own(1), lambda i: n_o(i, p.y, 1), lambda i, s: half(n_o(i, p.y, 1), s), p.z, p.Z(1), p.Z(-1), t0, u1)
    loc = [cm.local(own(k), n_o(p.z, p.y, k)) for k in range(2)]
    for t, _ in zip(ya, zb):
        yield t
    list(zb)
    for v in loc:
        v.wait()
    t1 = t0 + 1.5 * u1 + 2.0
    al, h2 = slice(None), lambda s: pl.ds(2 * s, 2)
    za = ring_ag(cm, n_o(p.z, al, 0), lambda i: n_o(i, al, 0), lambda i, s: n_o(i, h2(s), 0), p.z, p.Z(1), p.Z(-1), t1, u2)
    yb = ring_ag(cm, n_o(al, p.y, 1), lambda i: n_o(al, i, 1), lambda i, s: n_o(h2(s), i, 1), p.y, p.Y(1), p.Y(-1), t1, u2)
    for t, _ in zip(za, yb):
        yield t
    list(yb)


def ring_rs(cm, get, r1p, r1m, ap, am, fp, fm, res, m, plus, minus, t0, u):
    lo, hi, far = (m + 3) % 4, (m + 1) % 4, (m + 2) % 4
    hb = r1p.shape[-2]
    f0, f1 = (Ellipsis, pl.ds(0, hb), slice(None)), (Ellipsis, pl.ds(hb, hb), slice(None))
    p0 = cm.send(get(far, 0), r1p, plus)
    m0 = cm.send(get(far, 1), r1m, minus)
    p1 = cm.send(get(hi, 1), fp.at[f1], plus)
    m1 = cm.send(get(lo, 0), fm.at[f0], minus)
    yield t0 + 0.5 * u
    p0.wait_recv()
    ap[...] = r1p[...] + get(hi, 0)[...]
    p2 = cm.send(ap, fp.at[f0], plus)
    m0.wait_recv()
    am[...] = r1m[...] + get(lo, 1)[...]
    m2 = cm.send(am, fm.at[f1], minus)
    yield t0 + u
    p1.wait_recv()
    m1.wait_recv()
    yield t0 + 1.5 * u
    p2.wait_recv()
    m2.wait_recv()
    res[f0] = (fp[f0] + fm[f0]) + get(m, 0)[...]
    res[f1] = (fp[f1] + fm[f1]) + get(m, 1)[...]


def block(x, g, wg, wu, wd, o, wo, wq, x_o, q_o,
          xs, gb, nb, n, wgb, wub, wdb, wob, wqb, ov, a1, a2, y,
          r1, c1, f1, s1, r2, c2, f2, s2, xn, xr, nh, n1, qk, xq, ssem, rsem, lsem):
    p = Pos()
    cm = Comm(ssem, rsem, lsem)
    barrier([p.H(d) for d in range(1, 8)] + [p.Y(1), p.Y(-1), p.Z(1), p.Z(-1)])
    tb, dh = xs.shape[1:]
    ww = wgb.shape[2]
    d = n.shape[3]
    dc = d // 2
    hb = tb // 2
    qb = hb // 2
    al = slice(None)

    def dyn(i, m):
        return pl.ds(pl.multiple_of(i * m, m), m)

    def rows(q):
        return x.at[pl.ds(pl.multiple_of(1024 * q + tb * p.f, tb), tb), :]

    xin = []
    for k in range(1, 8):
        t = p.H(k)
        xin.append(cm.send(rows(quarter(t[1])), xs.at[p.h], t))
        xin.append(cm.send(g, gb.at[p.h], t))
    loc = [cm.local(rows(p.q), xs.at[p.h]), cm.local(g, gb.at[p.h])]

    def cols(w, j):
        return w.at[:, dyn(j, ww)]

    def slot(b, h):
        return b.at[:, dyn(h % 4, dh)]

    down_in, late, got = [], [], []

    def weights():
        ws = ((wg, wgb), (wu, wub))
        own, b, a, c, a2_ = [], [], [], [], []
        for w, wb in ws:
            b.append(cm.send(cols(w, 1 - p.j), wb.at[p.h], p.B))
            a.append(cm.send(cols(w, p.j), wb.at[p.h], p.A))
            c.append(cm.send(cols(w, p.j), wb.at[p.h], p.C))
            own.append(cm.local(cols(w, p.j), wb.at[p.h]))
        own.append(cm.local(o.at[pl.ds(pl.multiple_of(1024 * p.q, 1024), 1024), :], ov))
        for w, wb in ((wd, wdb), (wo, wob)):
            own.append(cm.local(w, slot(wb, p.h)))
        own.append(cm.local(wq, wqb.at[p.h]))
        for k, (w, wb) in enumerate(ws):
            yield 17.0 + 12.5 * k
            b[k].wait_recv()
            s = wb.at[p.B[1]]
            a2_.append(cm.send(s, s, p.A))
            c.append(cm.send(s, s, p.C))
            a[k].wait_recv()
            s = wb.at[p.A[1]]
            c.append(cm.send(s, s, p.C))
        for w, wb in ((wd, wdb), (wo, wob)):
            down_in.append(cm.send(w, slot(wb, p.h), p.A))
            late.append(cm.send(w, slot(wb, p.h), p.C))
        for k, (w, wb) in enumerate(ws):
            yield 46.0 + 12.5 * k
            a2_[k].wait_recv()
            s = wb.at[(2 * (3 - p.A[1] // 2)) + p.c]
            c.append(cm.send(s, s, p.C))
        yield 60.0
        for v in c:
            v.wait_recv()
        for v in own:
            v.wait()

    def tokens():
        yield 5.0
        for v in xin:
            v.wait_recv()
        for v in loc:
            v.wait()
        ss = jnp.zeros((tb, 1), F32)
        for k in range(8):
            v = xs[k].astype(F32)
            ss = ss + jnp.sum(v * v, axis=-1, keepdims=True)
        r = lax.rsqrt(ss / float(d) + EPS)
        for k in range(8):
            nb[:, dh * k:dh * (k + 1)] = (xs[k].astype(F32) * r * gb[k, 0:1, :]).astype(BF)
        part = (pl.ds(0, dc), pl.ds(dc, dc))
        yield from plane_ag(cm, p, lambda k: nb.at[:, part[k]], lambda zi, yi, k: n.at[zi, yi, :, part[k]],
                            lambda v, s: v.at[pl.ds(hb * s, hb), :], 13.0, 6.0, 17.0)

    run(tokens(), weights())

    tn = 256
    for b in range(4):
        s, zh = b // 2, b % 2

        def gate_up(t, carry, b=b, s=s, zh=zh):
            v = n[2 * zh:2 * zh + 2, :, hb * s:hb * (s + 1), :].reshape(8 * hb, d)
            cs = dyn(t, tn)
            gt = _dot(v, wgb[:, :, cs].reshape(d, tn))
            up = _dot(v, wub[:, :, cs].reshape(d, tn))
            a1[b, :, cs] = (jax.nn.silu(gt) * up).astype(BF)
            return carry

        lax.fori_loop(0, ww // tn, gate_up, 0)
        got.append(cm.send(a1.at[b], a2.at[b], p.B))

    qc = []
    m = p.x
    lo, hi, far = (m + 3) % 4, (m + 1) % 4, (m + 2) % 4

    def qweights():
        def blk(i):
            return wqb.at[2 * i + p.c]

        hr = wq.shape[0] // 2

        def half(i, s):
            return wqb.at[2 * i + p.c, pl.ds(hr * s, hr), :]

        p0 = cm.send(wq, blk(m), p.H(2))
        m0 = cm.send(wq, blk(m), p.H(-2))
        qc.append(cm.send(wq, blk(m), p.C))
        yield 112.0
        p0.wait_recv()
        p1 = cm.send(half(lo, 0), half(lo, 0), p.H(2))
        qc.append(cm.send(blk(lo), blk(lo), p.C))
        m0.wait_recv()
        m1 = cm.send(half(hi, 1), half(hi, 1), p.H(-2))
        qc.append(cm.send(blk(hi), blk(hi), p.C))
        yield 120.0
        p1.wait_recv()
        m1.wait_recv()
        qc.append(cm.send(blk(far), blk(far), p.C))
        yield 127.0
        for v in qc:
            v.wait_recv()

    kn = 512

    def down(b):
        s, zh = b // 2, b % 2
        got[b].wait_recv()

        def step(t, carry):
            cs = dyn(t, kn)
            ob = ov[512 * zh:512 * (zh + 1), :].reshape(8, tb, -1)[:, hb * s:hb * (s + 1), :].reshape(8 * hb, -1)
            v = (_dot(a1[b], wdb[dyn(p.j, ww), cs]) + _dot(a2[b], wdb[dyn(1 - p.j, ww), cs]) + _dot(ob, wob[:, cs]))
            y[s, 2 * zh:2 * zh + 2, :, :, cs] = v.reshape(2, 4, hb, kn)
            return carry

        lax.fori_loop(0, wdb.shape[1] // kn, step, 0)

    xex = []

    def chain(s, t0):
        if s == 0:
            yield 84.0
            for v, wb in zip(down_in, (wdb, wob)):
                v.wait_recv()
                sl = slot(wb, p.A[1])
                late.append(cm.send(sl, sl, p.C))
            yield 87.0
            for v in late:
                v.wait_recv()
        else:
            yield t0 - 8.0
        down(2 * s)
        yield t0 - 2.0
        down(2 * s + 1)
        ca, cb = pl.ds(0, dc // 2), pl.ds(dc // 2, dc // 2)

        def both(get_a, get_b, r, c, f, res, ax_a, ax_b, t, u):
            ga = ring_rs(cm, get_a, r.at[s, 0], r.at[s, 1], c.at[s, 0], c.at[s, 1], f.at[s, 0], f.at[s, 1],
                         res.at[s, 0], *ax_a, t, u)
            gb_ = ring_rs(cm, get_b, r.at[s, 2], r.at[s, 3], c.at[s, 2], c.at[s, 3], f.at[s, 2], f.at[s, 3],
                          res.at[s, 1], *ax_b, t, u)
            for v, _ in zip(ga, gb_):
                yield v
            list(gb_)

        ay, az = (p.y, p.Y(1), p.Y(-1)), (p.z, p.Z(1), p.Z(-1))
        yield from both(lambda i, k: y.at[s, :, i, pl.ds(qb * k, qb), ca], lambda i, k: y.at[s, i, :, pl.ds(qb * k, qb), cb],
                        r1, c1, f1, s1, ay, az, t0 + 1.5, 8.5)
        yield from both(lambda i, k: s1.at[s, 0, i, pl.ds(qb * k, qb), :], lambda i, k: s1.at[s, 1, i, pl.ds(qb * k, qb), :],
                        r2, c2, f2, s2, az, ay, t0 + 14.5, 3.0)
        t = t0 + 20.0
        rs = pl.ds(hb * s, hb)
        for k in range(4):
            yk = s2[s, k // 2, :, dh * (k % 2):dh * (k % 2 + 1)]
            xn[s, :, dh * k:dh * (k + 1)] = (xs[4 * p.j + k, rs, :].astype(F32) + yk).astype(BF)
        ex = cm.send(xn.at[s, dyn(1 - p.j, qb), :], xr.at[s], p.B)
        for v in (p.A, p.C, p.AC):
            xex.append(cm.send(xn.at[s, :, dyn(v[1] % 4, dh)], xq.at[p.q, rs, :], v).wait_recv)
        xex.append(cm.local(xn.at[s, :, dyn(p.h % 4, dh)], xq.at[p.q, rs, :]).wait)
        mine = xn[s, dyn(p.j, qb), :].astype(F32)
        yield t + 2.0
        ex.wait_recv()
        oth = xr[s].astype(F32)
        ss = jnp.sum(mine * mine, axis=-1, keepdims=True) + jnp.sum(oth * oth, axis=-1, keepdims=True)
        r = lax.rsqrt(ss / float(d) + EPS)
        for k in range(4):
            cs = slice(dh * k, dh * (k + 1))
            nh[s, p.j, :, cs] = (mine[:, cs] * r * gb[4 * p.j + k, 1:2, :]).astype(BF)
            nh[s, 1 - p.j, :, cs] = (oth[:, cs] * r * gb[4 * (1 - p.j) + k, 1:2, :]).astype(BF)
        part = (pl.ds(0, dc), pl.ds(dc, dc))
        hd = dc // 2
        yield from plane_ag(cm, p, lambda k: nh.at[s, k], lambda zi, yi, k: n1.at[s, zi, yi, :, part[k]],
                            lambda v, k: v.at[:, pl.ds(hd * k, hd)], t + 3.0, 2.5, 6.0)
        yield t + 20.0

        if s == 0:
            for _ in qw:
                pass

        def proj(t_, carry):
            cs = dyn(t_, tn)
            qk[s, :, :, cs] = _dot(n1[s].reshape(16 * qb, d), wqb[:, :, cs].reshape(d, tn)).astype(BF).reshape(16, qb, tn)
            return carry

        lax.fori_loop(0, wq.shape[1] // tn, proj, 0)

        def blk(xx):
            h = 2 * xx + p.c
            return q_o.at[quarter(h), :, s, h // 4]

        def half(xx, k):
            h = 2 * xx + p.c
            return q_o.at[quarter(h), pl.ds(8 * k, 8), s, h // 4]

        own = cm.local(qk.at[s], blk(m))
        p0 = cm.send(qk.at[s], blk(m), p.H(2))
        m0 = cm.send(qk.at[s], blk(m), p.H(-2))
        c = [cm.send(qk.at[s], blk(m), p.C)]
        yield t + 31.0
        p0.wait_recv()
        p1 = cm.send(half(lo, 0), half(lo, 0), p.H(2))
        m0.wait_recv()
        m1 = cm.send(half(hi, 1), half(hi, 1), p.H(-2))
        for b in (blk(lo), blk(hi)):
            c.append(cm.send(b, b, p.C))
        yield t + 38.0
        p1.wait_recv()
        c.append(cm.send(half(far, 0), half(far, 0), p.C))
        m1.wait_recv()
        c.append(cm.send(half(far, 1), half(far, 1), p.C))
        yield t + 42.0
        own.wait()
        for v in c:
            v.wait_recv()

    def resid():
        yield 134.0
        for wait in xex:
            wait()
        yield from plane_ag(cm, p, lambda k: xq.at[pl.ds(2 * k, 2)], lambda zi, yi, k: x_o.at[pl.ds(2 * k, 2), zi, yi],
                            lambda v, k: v.at[k], 138.0, 3.0, 10.0)

    def qrest():
        yield next(qw)
        yield from qw

    qw = qweights()
    run(qrest(), chain(0, 91.0), chain(1, 103.0), resid())
    cm.finish()


def solution(mesh):
    def body(x, g1, g2, w_gate, w_up, w_down, o, w_o, w_qkv):
        t, dh = x.shape
        d = dh * 8
        ff = w_gate.shape[1]
        tq = t // 4
        tb = tq // 16
        fh = ff // 2
        hb, qb, w2, nq = tb // 2, tb // 4, d // 4, w_qkv.shape[1]
        g = jnp.concatenate([jnp.stack([g1, g2]), jnp.zeros((6, dh), F32)], axis=0)
        bf, f32 = (lambda *v: pltpu.VMEM(v, BF)), (lambda *v: pltpu.VMEM(v, F32))
        ns = 208
        xo, qo = pl.pallas_call(
            block,
            out_shape=[jax.ShapeDtypeStruct((4, 4, 4, tb, dh), BF), jax.ShapeDtypeStruct((4, 16, 2, 2, qb, nq), BF)],
            in_specs=[HB] * 8,
            out_specs=[ANY] * 2,
            scratch_shapes=[
                bf(8, tb, dh), f32(8, 8, dh), bf(tb, d), bf(4, 4, tb, d), bf(8, dh, fh), bf(8, dh, fh),
                bf(ff, d // 2), bf(w_o.shape[0], d // 2), bf(8, dh, nq), bf(tq, w_o.shape[0]),
                bf(4, tq // 4, fh), bf(4, tq // 4, fh), f32(2, 4, 4, hb, d // 2),
                f32(2, 4, 4, qb, w2), f32(2, 4, 4, qb, w2), f32(2, 4, 4, hb, w2), f32(2, 2, 4, hb, w2),
                f32(2, 4, qb, w2), f32(2, 4, qb, w2), f32(2, 4, hb, w2), f32(2, 2, hb, w2),
                bf(2, hb, d // 2), bf(2, qb, d // 2), bf(2, 2, qb, d // 2), bf(2, 4, 4, qb, d), bf(2, 16, qb, nq),
                bf(4, tb, dh),
                pltpu.SemaphoreType.DMA((ns,)), pltpu.SemaphoreType.DMA((ns,)), pltpu.SemaphoreType.DMA((28,))],
            compiler_params=pltpu.CompilerParams(collective_id=1, has_side_effects=True,
                                                 vmem_limit_bytes=63 * 1024 * 1024),
            name='block',
        )(x, g, w_gate, w_up, w_down, o, w_o, w_qkv)
        return xo.reshape(t, dh), qo.reshape(t, -1)

    in_specs = (P(None, 'h'), P('h'), P('h'), P('h', 'f'), P('h', 'f'), P('f', 'h'),
                P(None, 'f'), P('f', 'h'), P('h', 'f'))
    return jax.shard_map(body, mesh=mesh, in_specs=in_specs,
                         out_specs=(P(None, 'h'), P(None, 'f')), check_vma=False)
```

time: 884 us -> 204 us (0.23)
  waiting for transfers between devices: 622 us -> 0 us
  Pallas kernels: 0 us -> 193 us
  blocking collectives: 180 us -> 0 us
  matrix products: 57.5 us -> 0 us
  between operations: 14.1 us -> 0.66 us
    psum x2 -> x0, waiting for transfers between devices: 622 us -> none  [the longest x1 500 us: body(): gt, up = lax.psum((_dot(n, w_gate), _dot(n, w_up)), 'h')]
    pallas_call x0 -> x1, Pallas kernels: none -> 193 us  [body(): pl.pallas_call(block, out_shape=[jax.ShapeDtypeStruct((4, 4, 4, tb, dh),...]
    psum x3 -> x0, blocking collectives: 180 us -> none  [the longest x1 134 us: body(): qkv = lax.psum(_dot(n1, w_qkv), 'h').astype(jnp.bfloat16)]
    dot_general x5 -> x0, matrix products: 57.5 us -> none  [_dot(): return jnp.dot(a, b, preferred_element_type=jnp.float32)]
    reduce_sum x2 -> x0, other arithmetic: 9.05 us -> none  [_norm(): ss = lax.psum(jnp.sum(xf * xf, axis=-1, keepdims=True), 'h')]
  transfers between devices with their start and end apart: 2 -> 0, of which waited for: 2 -> 0; matrix products, arithmetic and copies ran while one was open for 0% -> 0% of each run, Pallas kernels for 0% -> 0%
where the time goes in v4:
time: 204 us; the launch traced here: 203 us
  Pallas kernels  193 us (95%)
  local copies, waits for them, and re-layouts  8.82 us (4%)
    pallas_call x1, Pallas kernels, body(): pl.pallas_call(block, out_shape=[jax.ShapeDtypeStruct((4, 4, 4, tb, dh),...  193 us
    unnamed x4, local copies, waits for them, and re-layouts  7.37 us

profile of v4, /device:TPU:1, one launch (start us, length us, event | category | flops | bytes accessed | tf_op | source)
XLA Modules:
  0.0 203.4 jit_solution(9853490580651936364)
XLA Ops:
  0.6 0.1 pad.2.clone
  0.7 0.7 stack.6
  1.4 0.7 stack.7
  2.1 0.7 maximum_maximum_fusion.g
  2.8 193.2 %block.1 = (bf16[4,4,4,64,384]{4,3,2,1,0:T(8,128)(2,1)}, bf16[4,16,2,2,16,768]{5,4,3,2,1,0:T(8,128)(2,1)}) custom-call(bf16[4096,384]{1,0:T(8,128)(2,1)} %x.1, f32[8,384]{1,0:T(8,128)} %maximum_maximum_fusion.g, bf16[384,1536]{1,0:T(8,128)(2,1)} %wg.1, bf16[384,1536]{1,0:T(8,128)(2,1)} %wu.1, bf16[1536,384]{1,0:T(8,128)(2,1)} %wd.1, bf16[4096,256]{1,0:T(8,128)(2,1)} %o.1, ...), custom_call_target="tpu_custom_call" | custom-call | tf_op jit(solution)/shard_map/block/pallas_call | solution.py:433
  196.0 0.0 copy-start
  196.0 4.0 %copy.13 = bf16[4096,384]{1,0:T(8,128)(2,1)} copy(bf16[4096,384]{1,0:T(8,128)(2,1)} %bitcast.3) | data formatting | bytes 6291456
  200.0 0.7 copy-done
  200.7 2.7 %copy.14 = bf16[4096,768]{1,0:T(8,128)(2,1)} copy(bf16[4096,768]{1,0:T(8,128)(2,1)S(1)} %bitcast.2) | data formatting | bytes 12582912
  (1 shorter events, 0.0 us)
Async XLA Ops:
  196.0 4.7 %copy-start = (bf16[4,16,2,2,16,768]{5,4,3,2,1,0:T(8,128)(2,1)S(1)}, bf16[4,16,2,2,16,768]{5,4,3,2,1,0:T(8,128)(2,1)}, u32[]{:S(2)}) copy-start(bf16[4,16,2,2,16,768]{5,4,3,2,1,0:T(8,128)(2,1)} %get-tuple-element.5) | copy-start | bytes 18874372

commit v5 on v4

--- a/solution.py
+++ b/solution.py
@@ -8,6 +8,7 @@
 from jax.sharding import PartitionSpec as P
 
 EPS = 1e-6
+VLIM = 56 * 1024 * 1024
 MESH = pl.DeviceIdType.MESH
 ANY = pl.BlockSpec(memory_space=pl.ANY)
 VM = pl.BlockSpec(memory_space=pltpu.VMEM)
@@ -75,6 +76,20 @@
             c.wait_send()
 
 
+class Part(Comm):
+    def __init__(self, cm):
+        self.cm = cm
+        self.sent = []
+
+    def send(self, src, dst, dev):
+        c = self.cm.send(src, dst, dev)
+        self.sent.append(self.cm.sent.pop())
+        return c
+
+    def local(self, src, dst):
+        return self.cm.local(src, dst)
+
+
 def barrier(devs):
     b = pltpu.get_barrier_semaphore()
     for d in devs:
@@ -111,16 +126,27 @@
     m1.wait_recv()
 
 
+def ring_direct(cm, own, blk, m, sides, t0, u):
+    c = [cm.send(own, blk(m), v) for v in sides]
+    yield t0 + u
+    for v in c:
+        v.wait_recv()
+
+
 def plane_ag(cm, p, own, n_o, half, t0, u1, u2):
-    ya = ring_ag(cm, own(0), lambda i: n_o(p.z, i, 0), lambda i, s: half(n_o(p.z, i, 0), s), p.y, p.Y(1), p.Y(-1), t0, u1)
-    zb = ring_ag(cm, own(1), lambda i: n_o(i, p.y, 1), lambda i, s: half(n_o(i, p.y, 1), s), p.z, p.Z(1), p.Z(-1), t0, u1)
+    if half is None:
+        ya = ring_direct(cm, own(0), lambda i: n_o(p.z, i, 0), p.y, (p.Y(1), p.Y(-1), p.Y(2)), t0, u1)
+        zb = ring_direct(cm, own(1), lambda i: n_o(i, p.y, 1), p.z, (p.Z(1), p.Z(-1), p.Z(2)), t0, u1)
+    else:
+        ya = ring_ag(cm, own(0), lambda i: n_o(p.z, i, 0), lambda i, s: half(n_o(p.z, i, 0), s), p.y, p.Y(1), p.Y(-1), t0, u1)
+        zb = ring_ag(cm, own(1), lambda i: n_o(i, p.y, 1), lambda i, s: half(n_o(i, p.y, 1), s), p.z, p.Z(1), p.Z(-1), t0, u1)
     loc = [cm.local(own(k), n_o(p.z, p.y, k)) for k in range(2)]
     for t, _ in zip(ya, zb):
         yield t
     list(zb)
     for v in loc:
         v.wait()
-    t1 = t0 + 1.5 * u1 + 2.0
+    t1 = t0 + (u1 if half is None else 1.5 * u1 + 2.0)
     al, h2 = slice(None), lambda s: pl.ds(2 * s, 2)
     za = ring_ag(cm, n_o(p.z, al, 0), lambda i: n_o(i, al, 0), lambda i, s: n_o(i, h2(s), 0), p.z, p.Z(1), p.Z(-1), t1, u2)
     yb = ring_ag(cm, n_o(al, p.y, 1), lambda i: n_o(al, i, 1), lambda i, s: n_o(h2(s), i, 1), p.y, p.Y(1), p.Y(-1), t1, u2)
@@ -129,7 +155,7 @@
     list(yb)
 
 
-def ring_rs(cm, get, r1p, r1m, ap, am, fp, fm, res, m, plus, minus, t0, u):
+def ring_rs(cm, get, r1p, r1m, fp, fm, res, m, plus, minus, t0, u):
     lo, hi, far = (m + 3) % 4, (m + 1) % 4, (m + 2) % 4
     hb = r1p.shape[-2]
     f0, f1 = (Ellipsis, pl.ds(0, hb), slice(None)), (Ellipsis, pl.ds(hb, hb), slice(None))
@@ -139,27 +165,29 @@
     m1 = cm.send(get(lo, 0), fm.at[f0], minus)
     yield t0 + 0.5 * u
     p0.wait_recv()
-    ap[...] = r1p[...] + get(hi, 0)[...]
-    p2 = cm.send(ap, fp.at[f0], plus)
+    v = get(hi, 0)
+    v[...] = r1p[...] + v[...]
+    p2 = cm.send(v, fp.at[f0], plus)
     m0.wait_recv()
-    am[...] = r1m[...] + get(lo, 1)[...]
-    m2 = cm.send(am, fm.at[f1], minus)
+    v = get(lo, 1)
+    v[...] = r1m[...] + v[...]
+    m2 = cm.send(v, fm.at[f1], minus)
     yield t0 + u
     p1.wait_recv()
     m1.wait_recv()
     yield t0 + 1.5 * u
     p2.wait_recv()
     m2.wait_recv()
-    res[f0] = (fp[f0] + fm[f0]) + get(m, 0)[...]
-    res[f1] = (fp[f1] + fm[f1]) + get(m, 1)[...]
+    res(0)[...] = (fp[f0] + fm[f0]) + get(m, 0)[...]
+    res(1)[...] = (fp[f1] + fm[f1]) + get(m, 1)[...]
 
 
 def block(x, g, wg, wu, wd, o, wo, wq, x_o, q_o,
           xs, gb, nb, n, wgb, wub, wdb, wob, wqb, ov, a1, a2, y,
-          r1, c1, f1, s1, r2, c2, f2, s2, xn, xr, nh, n1, qk, xq, ssem, rsem, lsem):
+          r1, f1, r2, f2, s2, xn, xr, nh, qk, xq, ssem, rsem, lsem):
     p = Pos()
     cm = Comm(ssem, rsem, lsem)
-    barrier([p.H(d) for d in range(1, 8)] + [p.Y(1), p.Y(-1), p.Z(1), p.Z(-1)])
+    barrier([p.H(k) for k in range(1, 8)] + [p.Y(k) for k in range(1, 4)] + [p.Z(k) for k in range(1, 4)])
     tb, dh = xs.shape[1:]
     ww = wgb.shape[2]
     d = n.shape[3]
@@ -181,48 +209,73 @@
         xin.append(cm.send(g, gb.at[p.h], t))
     loc = [cm.local(rows(p.q), xs.at[p.h]), cm.local(g, gb.at[p.h])]
 
-    def cols(w, j):
-        return w.at[:, dyn(j, ww)]
+    cw = ((0, 512), (512, 256))
+
+    def cols(w, j, k):
+        return w.at[:, pl.ds(pl.multiple_of(ww * j + cw[k][0], 128), cw[k][1])]
+
+    def part_of(b, h, k):
+        return b.at[h, :, pl.ds(*cw[k])]
 
     def slot(b, h):
         return b.at[:, dyn(h % 4, dh)]
 
-    down_in, late, got = [], [], []
+    down_in, late, got, own = [], [], [[], []], []
+    cn = Part(cm)
+    ready = [[], []]
 
     def weights():
         ws = ((wg, wgb), (wu, wub))
-        own, b, a, c, a2_ = [], [], [], [], []
-        for w, wb in ws:
-            b.append(cm.send(cols(w, 1 - p.j), wb.at[p.h], p.B))
-            a.append(cm.send(cols(w, p.j), wb.at[p.h], p.A))
-            c.append(cm.send(cols(w, p.j), wb.at[p.h], p.C))
-            own.append(cm.local(cols(w, p.j), wb.at[p.h]))
+        fb, fa, f2_ = [[], []], [[], []], [[], []]
+        opp = 2 * (3 - p.A[1] // 2) + p.c
+
+        def fan(k, to_b, to_a):
+            for w, wb in ws:
+                dst = part_of(wb, p.h, k)
+                if to_b:
+                    fb[k].append(cm.send(cols(w, 1 - p.j, k), dst, p.B))
+                if to_a:
+                    fa[k].append(cm.send(cols(w, p.j, k), dst, p.A))
+                    ready[k].append(cm.send(cols(w, p.j, k), dst, p.C).wait_recv)
+                    ready[k].append(cm.local(cols(w, p.j, k), dst).wait)
+
+        def take(c, wb, h, k, onward):
+            c.wait_recv()
+            v = part_of(wb, h, k)
+            if onward:
+                f2_[k].append(cm.send(v, v, p.A))
+            ready[k].append(cm.send(v, v, p.C).wait_recv)
+
+        fan(0, True, True)
+        fan(1, True, False)
         own.append(cm.local(o.at[pl.ds(pl.multiple_of(1024 * p.q, 1024), 1024), :], ov))
         for w, wb in ((wd, wdb), (wo, wob)):
             own.append(cm.local(w, slot(wb, p.h)))
         own.append(cm.local(wq, wqb.at[p.h]))
-        for k, (w, wb) in enumerate(ws):
-            yield 17.0 + 12.5 * k
-            b[k].wait_recv()
-            s = wb.at[p.B[1]]
-            a2_.append(cm.send(s, s, p.A))
-            c.append(cm.send(s, s, p.C))
-            a[k].wait_recv()
-            s = wb.at[p.A[1]]
-            c.append(cm.send(s, s, p.C))
-        for w, wb in ((wd, wdb), (wo, wob)):
-            down_in.append(cm.send(w, slot(wb, p.h), p.A))
-            late.append(cm.send(w, slot(wb, p.h), p.C))
-        for k, (w, wb) in enumerate(ws):
-            yield 46.0 + 12.5 * k
-            a2_[k].wait_recv()
-            s = wb.at[(2 * (3 - p.A[1] // 2)) + p.c]
-            c.append(cm.send(s, s, p.C))
-        yield 60.0
-        for v in c:
-            v.wait_recv()
-        for v in own:
-            v.wait()
+        for k in range(2):
+            yield 14.0 + 8.0 * k
+            take(fb[0][k], ws[k][1], p.B[1], 0, True)
+            take(fa[0][k], ws[k][1], p.A[1], 0, False)
+        fan(1, False, True)
+        yield 31.0
+        for k in range(2):
+            take(fb[1][k], ws[k][1], p.B[1], 1, True)
+        hk = wd.shape[0] // 2
+        down_in.append((cm.send(wo, slot(wob, p.h), p.A), slot(wob, p.A[1])))
+        late.append(cm.send(wo, slot(wob, p.h), p.C))
+        for r in range(2):
+            down_in.append((cm.send(wd.at[pl.ds(hk * r, hk), :], slot(wdb, p.h).at[pl.ds(hk * r, hk), :], p.A),
+                            slot(wdb, p.A[1]).at[pl.ds(hk * r, hk), :]))
+        late.append(cm.send(wd, slot(wdb, p.h), p.C))
+        for k in range(2):
+            yield 34.0 + 7.0 * k
+            take(f2_[0][k], ws[k][1], opp, 0, False)
+        yield 49.0
+        for k in range(2):
+            take(fa[1][k], ws[k][1], p.A[1], 1, False)
+        for k in range(2):
+            yield 56.0 + 4.5 * k
+            take(f2_[1][k], ws[k][1], opp, 1, False)
 
     def tokens():
         yield 5.0
@@ -238,25 +291,42 @@
         for k in range(8):
             nb[:, dh * k:dh * (k + 1)] = (xs[k].astype(F32) * r * gb[k, 0:1, :]).astype(BF)
         part = (pl.ds(0, dc), pl.ds(dc, dc))
-        yield from plane_ag(cm, p, lambda k: nb.at[:, part[k]], lambda zi, yi, k: n.at[zi, yi, :, part[k]],
-                            lambda v, s: v.at[pl.ds(hb * s, hb), :], 13.0, 6.0, 17.0)
-
-    run(tokens(), weights())
+        yield from plane_ag(cn, p, lambda k: nb.at[:, part[k]], lambda zi, yi, k: n.at[zi, yi, :, part[k]],
+                            lambda v, s: v.at[pl.ds(hb * s, hb), :], 13.0, 6.0, 16.0)
 
     tn = 256
-    for b in range(4):
+
+    def gate_up(k, b):
         s, zh = b // 2, b % 2
 
-        def gate_up(t, carry, b=b, s=s, zh=zh):
+        def step(t, carry):
             v = n[2 * zh:2 * zh + 2, :, hb * s:hb * (s + 1), :].reshape(8 * hb, d)
-            cs = dyn(t, tn)
+            cs = pl.ds(pl.multiple_of(cw[k][0] + t * tn, tn), tn)
             gt = _dot(v, wgb[:, :, cs].reshape(d, tn))
             up = _dot(v, wub[:, :, cs].reshape(d, tn))
             a1[b, :, cs] = (jax.nn.silu(gt) * up).astype(BF)
             return carry
 
-        lax.fori_loop(0, ww // tn, gate_up, 0)
-        got.append(cm.send(a1.at[b], a2.at[b], p.B))
+        lax.fori_loop(0, cw[k][1] // tn, step, 0)
+        got[k].append(cm.send(part_of(a1, b, k), part_of(a2, b, k), p.B))
+
+    def first():
+        yield from tokens()
+        yield 47.5
+        for wait in ready[0]:
+            wait()
+        for b in range(4):
+            gate_up(0, b)
+            yield 51.0 + 2.0 * b
+
+    run(first(), weights())
+    for wait in ready[1]:
+        wait()
+    for b in range(4):
+        gate_up(1, b)
+    for v in own:
+        v.wait()
+    cn.finish()
 
     qc = []
     m = p.x
@@ -293,7 +363,8 @@
 
     def down(b):
         s, zh = b // 2, b % 2
-        got[b].wait_recv()
+        for k in range(2):
+            got[k][b].wait_recv()
 
         def step(t, carry):
             cs = dyn(t, kn)
@@ -308,12 +379,11 @@
 
     def chain(s, t0):
         if s == 0:
-            yield 84.0
-            for v, wb in zip(down_in, (wdb, wob)):
+            for k, (v, sl) in enumerate(down_in):
+                yield 66.0 + 10.0 * k
                 v.wait_recv()
-                sl = slot(wb, p.A[1])
                 late.append(cm.send(sl, sl, p.C))
-            yield 87.0
+            yield 88.0
             for v in late:
                 v.wait_recv()
         else:
@@ -323,20 +393,21 @@
         down(2 * s + 1)
         ca, cb = pl.ds(0, dc // 2), pl.ds(dc // 2, dc // 2)
 
-        def both(get_a, get_b, r, c, f, res, ax_a, ax_b, t, u):
-            ga = ring_rs(cm, get_a, r.at[s, 0], r.at[s, 1], c.at[s, 0], c.at[s, 1], f.at[s, 0], f.at[s, 1],
-                         res.at[s, 0], *ax_a, t, u)
-            gb_ = ring_rs(cm, get_b, r.at[s, 2], r.at[s, 3], c.at[s, 2], c.at[s, 3], f.at[s, 2], f.at[s, 3],
-                          res.at[s, 1], *ax_b, t, u)
+        def both(get_a, get_b, r, f, res_a, res_b, ax_a, ax_b, t, u):
+            ga = ring_rs(cm, get_a, r.at[s, 0], r.at[s, 1], f.at[s, 0], f.at[s, 1], res_a, *ax_a, t, u)
+            gb_ = ring_rs(cm, get_b, r.at[s, 2], r.at[s, 3], f.at[s, 2], f.at[s, 3], res_b, *ax_b, t, u)
             for v, _ in zip(ga, gb_):
                 yield v
             list(gb_)
 
+        def rr(k):
+            return pl.ds(qb * k, qb)
+
         ay, az = (p.y, p.Y(1), p.Y(-1)), (p.z, p.Z(1), p.Z(-1))
-        yield from both(lambda i, k: y.at[s, :, i, pl.ds(qb * k, qb), ca], lambda i, k: y.at[s, i, :, pl.ds(qb * k, qb), cb],
-                        r1, c1, f1, s1, ay, az, t0 + 1.5, 8.5)
-        yield from both(lambda i, k: s1.at[s, 0, i, pl.ds(qb * k, qb), :], lambda i, k: s1.at[s, 1, i, pl.ds(qb * k, qb), :],
-                        r2, c2, f2, s2, az, ay, t0 + 14.5, 3.0)
+        yield from both(lambda i, k: y.at[s, :, i, rr(k), ca], lambda i, k: y.at[s, i, :, rr(k), cb], r1, f1,
+                        lambda k: y.at[s, :, p.y, rr(k), ca], lambda k: y.at[s, p.z, :, rr(k), cb], ay, az, t0 + 1.5, 8.5)
+        yield from both(lambda i, k: y.at[s, i, p.y, rr(k), ca], lambda i, k: y.at[s, p.z, i, rr(k), cb], r2, f2,
+                        lambda k: s2.at[s, 0, rr(k), :], lambda k: s2.at[s, 1, rr(k), :], az, ay, t0 + 14.5, 3.0)
         t = t0 + 20.0
         rs = pl.ds(hb * s, hb)
         for k in range(4):
@@ -357,9 +428,9 @@
             nh[s, p.j, :, cs] = (mine[:, cs] * r * gb[4 * p.j + k, 1:2, :]).astype(BF)
             nh[s, 1 - p.j, :, cs] = (oth[:, cs] * r * gb[4 * (1 - p.j) + k, 1:2, :]).astype(BF)
         part = (pl.ds(0, dc), pl.ds(dc, dc))
-        hd = dc // 2
-        yield from plane_ag(cm, p, lambda k: nh.at[s, k], lambda zi, yi, k: n1.at[s, zi, yi, :, part[k]],
-                            lambda v, k: v.at[:, pl.ds(hd * k, hd)], t + 3.0, 2.5, 6.0)
+        n1 = n.at[:, :, pl.ds(hb * s, qb), :]
+        yield from plane_ag(cm, p, lambda k: nh.at[s, k], lambda zi, yi, k: n1.at[zi, yi, :, part[k]],
+                            None, t + 3.0, 3.0, 6.0)
         yield t + 20.0
 
         if s == 0:
@@ -368,7 +439,7 @@
 
         def proj(t_, carry):
             cs = dyn(t_, tn)
-            qk[s, :, :, cs] = _dot(n1[s].reshape(16 * qb, d), wqb[:, :, cs].reshape(d, tn)).astype(BF).reshape(16, qb, tn)
+            qk[s, :, :, cs] = _dot(n[:, :, hb * s:hb * s + qb, :].reshape(16 * qb, d), wqb[:, :, cs].reshape(d, tn)).astype(BF).reshape(16, qb, tn)
             return carry
 
         lax.fori_loop(0, wq.shape[1] // tn, proj, 0)
@@ -407,14 +478,14 @@
         for wait in xex:
             wait()
         yield from plane_ag(cm, p, lambda k: xq.at[pl.ds(2 * k, 2)], lambda zi, yi, k: x_o.at[pl.ds(2 * k, 2), zi, yi],
-                            lambda v, k: v.at[k], 138.0, 3.0, 10.0)
+                            None, 134.0, 3.0, 10.0)
 
     def qrest():
         yield next(qw)
         yield from qw
 
     qw = qweights()
-    run(qrest(), chain(0, 91.0), chain(1, 103.0), resid())
+    run(qrest(), chain(0, 92.0), chain(1, 96.5), resid())
     cm.finish()
 
 
@@ -429,7 +500,7 @@
         hb, qb, w2, nq = tb // 2, tb // 4, d // 4, w_qkv.shape[1]
         g = jnp.concatenate([jnp.stack([g1, g2]), jnp.zeros((6, dh), F32)], axis=0)
         bf, f32 = (lambda *v: pltpu.VMEM(v, BF)), (lambda *v: pltpu.VMEM(v, F32))
-        ns = 208
+        ns = 216
         xo, qo = pl.pallas_call(
             block,
             out_shape=[jax.ShapeDtypeStruct((4, 4, 4, tb, dh), BF), jax.ShapeDtypeStruct((4, 16, 2, 2, qb, nq), BF)],
@@ -439,13 +510,12 @@
                 bf(8, tb, dh), f32(8, 8, dh), bf(tb, d), bf(4, 4, tb, d), bf(8, dh, fh), bf(8, dh, fh),
                 bf(ff, d // 2), bf(w_o.shape[0], d // 2), bf(8, dh, nq), bf(tq, w_o.shape[0]),
                 bf(4, tq // 4, fh), bf(4, tq // 4, fh), f32(2, 4, 4, hb, d // 2),
-                f32(2, 4, 4, qb, w2), f32(2, 4, 4, qb, w2), f32(2, 4, 4, hb, w2), f32(2, 2, 4, hb, w2),
-                f32(2, 4, qb, w2), f32(2, 4, qb, w2), f32(2, 4, hb, w2), f32(2, 2, hb, w2),
-                bf(2, hb, d // 2), bf(2, qb, d // 2), bf(2, 2, qb, d // 2), bf(2, 4, 4, qb, d), bf(2, 16, qb, nq),
+                f32(2, 4, 4, qb, w2), f32(2, 4, 4, hb, w2), f32(2, 4, qb, w2), f32(2, 4, hb, w2), f32(2, 2, hb, w2),
+                bf(2, hb, d // 2), bf(2, qb, d // 2), bf(2, 2, qb, d // 2), bf(2, 16, qb, nq),
                 bf(4, tb, dh),
                 pltpu.SemaphoreType.DMA((ns,)), pltpu.SemaphoreType.DMA((ns,)), pltpu.SemaphoreType.DMA((28,))],
             compiler_params=pltpu.CompilerParams(collective_id=1, has_side_effects=True,
-                                                 vmem_limit_bytes=63 * 1024 * 1024),
+                                                 vmem_limit_bytes=VLIM),
             name='block',
         )(x, g, w_gate, w_up, w_down, o, w_o, w_qkv)
         return xo.reshape(t, dh), qo.reshape(t, -1)

time: 204 us -> 207 us (1.015)
  Pallas kernels: 193 us -> 197 us
    pallas_call x1, Pallas kernels: 193 us -> 197 us  [body(): pl.pallas_call(block, out_shape=[jax.ShapeDtypeStruct((4, 4, 4, tb, dh),...]
where the time goes in v5:
time: 207 us
  Pallas kernels  197 us (95%)
  local copies, waits for them, and re-layouts  8.82 us (4%)
    pallas_call x1, Pallas kernels, body(): pl.pallas_call(block, out_shape=[jax.ShapeDtypeStruct((4, 4, 4, tb, dh),...  197 us
    unnamed x4, local copies, waits for them, and re-layouts  7.37 us

profile of v5, /device:TPU:1, one launch (start us, length us, event | category | flops | bytes accessed | tf_op | source)
XLA Modules:
  0.0 207.1 jit_solution(9747833212160792054)
XLA Ops:
  0.6 0.1 pad.2.clone
  0.7 0.7 stack.6
  1.4 0.7 stack.7
  2.1 0.7 maximum_maximum_fusion.g
  2.8 197.0 %block.1 = (bf16[4,4,4,64,384]{4,3,2,1,0:T(8,128)(2,1)}, bf16[4,16,2,2,16,768]{5,4,3,2,1,0:T(8,128)(2,1)}) custom-call(bf16[4096,384]{1,0:T(8,128)(2,1)} %x.1, f32[8,384]{1,0:T(8,128)} %maximum_maximum_fusion.g, bf16[384,1536]{1,0:T(8,128)(2,1)} %wg.1, bf16[384,1536]{1,0:T(8,128)(2,1)} %wu.1, bf16[1536,384]{1,0:T(8,128)(2,1)} %wd.1, bf16[4096,256]{1,0:T(8,128)(2,1)} %o.1, ...), custom_call_target="tpu_custom_call" | custom-call | tf_op jit(solution)/shard_map/block/pallas_call | solution.py:504
  199.7 0.0 copy-start
  199.8 4.0 %copy.13 = bf16[4096,384]{1,0:T(8,128)(2,1)} copy(bf16[4096,384]{1,0:T(8,128)(2,1)} %bitcast.3) | data formatting | bytes 6291456
  203.8 0.7 copy-done
  204.4 2.7 %copy.14 = bf16[4096,768]{1,0:T(8,128)(2,1)} copy(bf16[4096,768]{1,0:T(8,128)(2,1)S(1)} %bitcast.2) | data formatting | bytes 12582912
  (1 shorter events, 0.0 us)
Async XLA Ops:
  199.7 4.7 %copy-start = (bf16[4,16,2,2,16,768]{5,4,3,2,1,0:T(8,128)(2,1)S(1)}, bf16[4,16,2,2,16,768]{5,4,3,2,1,0:T(8,128)(2,1)}, u32[]{:S(2)}) copy-start(bf16[4,16,2,2,16,768]{5,4,3,2,1,0:T(8,128)(2,1)} %get-tuple-element.5) | copy-start | bytes 18874372

commit v6 on v5

--- a/solution.py
+++ b/solution.py
@@ -155,7 +155,7 @@
     list(yb)
 
 
-def ring_rs(cm, get, r1p, r1m, fp, fm, res, m, plus, minus, t0, u):
+def ring_rs(cm, get, r1p, r1m, fp, fm, res, m, plus, minus, t0, u, lat):
     lo, hi, far = (m + 3) % 4, (m + 1) % 4, (m + 2) % 4
     hb = r1p.shape[-2]
     f0, f1 = (Ellipsis, pl.ds(0, hb), slice(None)), (Ellipsis, pl.ds(hb, hb), slice(None))
@@ -163,7 +163,7 @@
     m0 = cm.send(get(far, 1), r1m, minus)
     p1 = cm.send(get(hi, 1), fp.at[f1], plus)
     m1 = cm.send(get(lo, 0), fm.at[f0], minus)
-    yield t0 + 0.5 * u
+    yield t0 + 0.5 * u + lat
     p0.wait_recv()
     v = get(hi, 0)
     v[...] = r1p[...] + v[...]
@@ -172,19 +172,26 @@
     v = get(lo, 1)
     v[...] = r1m[...] + v[...]
     m2 = cm.send(v, fm.at[f1], minus)
-    yield t0 + u
+    yield t0 + 1.5 * u + 2.0 * lat
     p1.wait_recv()
     m1.wait_recv()
-    yield t0 + 1.5 * u
     p2.wait_recv()
     m2.wait_recv()
     res(0)[...] = (fp[f0] + fm[f0]) + get(m, 0)[...]
     res(1)[...] = (fp[f1] + fm[f1]) + get(m, 1)[...]
 
 
+def ring_rs_direct(cm, get, r, res, m, sides, t0, u):
+    c = [cm.send(get((m + k + 1) % 4), r.at[k], v) for k, v in enumerate(sides)]
+    yield t0 + u
+    for v in c:
+        v.wait_recv()
+    res[...] = (r[0] + r[1]) + (r[2] + get(m)[...])
+
+
 def block(x, g, wg, wu, wd, o, wo, wq, x_o, q_o,
           xs, gb, nb, n, wgb, wub, wdb, wob, wqb, ov, a1, a2, y,
-          r1, f1, r2, f2, s2, xn, xr, nh, qk, xq, ssem, rsem, lsem):
+          r1, f1, r2, s2, xn, xr, nh, qk, xq, ssem, rsem, lsem):
     p = Pos()
     cm = Comm(ssem, rsem, lsem)
     barrier([p.H(k) for k in range(1, 8)] + [p.Y(k) for k in range(1, 4)] + [p.Z(k) for k in range(1, 4)])
@@ -359,60 +366,84 @@
         for v in qc:
             v.wait_recv()
 
-    kn = 512
-
-    def down(b):
+    w3 = wdb.shape[1] // 2
+    w4 = w3 // 2
+    odd = p.x % 2
+    xex = []
+
+    def down(b, e):
         s, zh = b // 2, b % 2
-        for k in range(2):
-            got[k][b].wait_recv()
+        if e == 0:
+            for k in range(2):
+                got[k][b].wait_recv()
+        base = w3 * (odd if e == 0 else 1 - odd)
 
         def step(t, carry):
-            cs = dyn(t, kn)
+            cs = pl.ds(pl.multiple_of(base + t * tn, tn), tn)
             ob = ov[512 * zh:512 * (zh + 1), :].reshape(8, tb, -1)[:, hb * s:hb * (s + 1), :].reshape(8 * hb, -1)
             v = (_dot(a1[b], wdb[dyn(p.j, ww), cs]) + _dot(a2[b], wdb[dyn(1 - p.j, ww), cs]) + _dot(ob, wob[:, cs]))
-            y[s, 2 * zh:2 * zh + 2, :, :, cs] = v.reshape(2, 4, hb, kn)
+            y[s, 2 * zh:2 * zh + 2, :, :, pl.ds(pl.multiple_of(w3 * e + t * tn, tn), tn)] = v.reshape(2, 4, hb, tn)
             return carry
 
-        lax.fori_loop(0, wdb.shape[1] // kn, step, 0)
-
-    xex = []
+        lax.fori_loop(0, w3 // tn, step, 0)
+
+    def rr(k):
+        return pl.ds(qb * k, qb)
+
+    ay, az = (p.y, p.Y(1), p.Y(-1)), (p.z, p.Z(1), p.Z(-1))
+
+    def scatter(s, e, t):
+        ca, cb = pl.ds(w3 * e, w4), pl.ds(w3 * e + w4, w4)
+
+        def both(get_a, get_b, r, f, res_a, res_b, ax_a, ax_b, t, u, v):
+            ga = ring_rs(cm, get_a, r.at[s, e, 0], r.at[s, e, 1], f.at[s, e, 0], f.at[s, e, 1], res_a, *ax_a, t, u, v)
+            gb_ = ring_rs(cm, get_b, r.at[s, e, 2], r.at[s, e, 3], f.at[s, e, 2], f.at[s, e, 3], res_b, *ax_b, t, u, v)
+            for q, _ in zip(ga, gb_):
+                yield q
+            list(gb_)
+
+        yield from both(lambda i, k: y.at[s, :, i, rr(k), ca], lambda i, k: y.at[s, i, :, rr(k), cb], r1, f1,
+                        lambda k: y.at[s, :, p.y, rr(k), ca], lambda k: y.at[s, p.z, :, rr(k), cb], ay, az, t, 3.0, 2.0)
+        y3, z3 = [p.Y(k) for k in (1, 2, 3)], [p.Z(k) for k in (1, 2, 3)]
+        ga = ring_rs_direct(cm, lambda i: y.at[s, i, p.y, :, ca], r2.at[s, e, 0], s2.at[s, e, 0], p.z, z3, t + 11.0, 4.0)
+        gb_ = ring_rs_direct(cm, lambda i: y.at[s, p.z, i, :, cb], r2.at[s, e, 1], s2.at[s, e, 1], p.y, y3, t + 11.0, 4.0)
+        for q, _ in zip(ga, gb_):
+            yield q
+        list(gb_)
+
+    def weights2():
+        for k, (v, sl) in enumerate(down_in):
+            yield (66.0, 75.0, 87.5)[k]
+            v.wait_recv()
+            late.append(cm.send(sl, sl, p.C))
+
+    def own_part(s, t0):
+        yield t0 - 2.0
+        if s == 0:
+            for v in late[:2]:
+                v.wait_recv()
+            del late[:2]
+        down(2 * s, 0)
+        yield t0
+        down(2 * s + 1, 0)
+        yield from scatter(s, 0, t0 + 1.0)
 
     def chain(s, t0):
+        yield t0 - 2.0
         if s == 0:
-            for k, (v, sl) in enumerate(down_in):
-                yield 66.0 + 10.0 * k
-                v.wait_recv()
-                late.append(cm.send(sl, sl, p.C))
-            yield 88.0
             for v in late:
                 v.wait_recv()
-        else:
-            yield t0 - 8.0
-        down(2 * s)
-        yield t0 - 2.0
-        down(2 * s + 1)
-        ca, cb = pl.ds(0, dc // 2), pl.ds(dc // 2, dc // 2)
-
-        def both(get_a, get_b, r, f, res_a, res_b, ax_a, ax_b, t, u):
-            ga = ring_rs(cm, get_a, r.at[s, 0], r.at[s, 1], f.at[s, 0], f.at[s, 1], res_a, *ax_a, t, u)
-            gb_ = ring_rs(cm, get_b, r.at[s, 2], r.at[s, 3], f.at[s, 2], f.at[s, 3], res_b, *ax_b, t, u)
-            for v, _ in zip(ga, gb_):
-                yield v
-            list(gb_)
-
-        def rr(k):
-            return pl.ds(qb * k, qb)
-
-        ay, az = (p.y, p.Y(1), p.Y(-1)), (p.z, p.Z(1), p.Z(-1))
-        yield from both(lambda i, k: y.at[s, :, i, rr(k), ca], lambda i, k: y.at[s, i, :, rr(k), cb], r1, f1,
-                        lambda k: y.at[s, :, p.y, rr(k), ca], lambda k: y.at[s, p.z, :, rr(k), cb], ay, az, t0 + 1.5, 8.5)
-        yield from both(lambda i, k: y.at[s, i, p.y, rr(k), ca], lambda i, k: y.at[s, p.z, i, rr(k), cb], r2, f2,
-                        lambda k: s2.at[s, 0, rr(k), :], lambda k: s2.at[s, 1, rr(k), :], az, ay, t0 + 14.5, 3.0)
-        t = t0 + 20.0
+        down(2 * s, 1)
+        down(2 * s + 1, 1)
+        yield from scatter(s, 1, t0 + 1.0)
+        for _ in owns[s]:
+            pass
+        t = t0 + 18.0
         rs = pl.ds(hb * s, hb)
-        for k in range(4):
-            yk = s2[s, k // 2, :, dh * (k % 2):dh * (k % 2 + 1)]
-            xn[s, :, dh * k:dh * (k + 1)] = (xs[4 * p.j + k, rs, :].astype(F32) + yk).astype(BF)
+        for e in range(2):
+            for k in range(2):
+                i = 2 * (odd if e == 0 else 1 - odd) + k
+                xn[s, :, dyn(i, dh)] = (xs[4 * p.j + i, rs, :].astype(F32) + s2[s, e, k]).astype(BF)
         ex = cm.send(xn.at[s, dyn(1 - p.j, qb), :], xr.at[s], p.B)
         for v in (p.A, p.C, p.AC):
             xex.append(cm.send(xn.at[s, :, dyn(v[1] % 4, dh)], xq.at[p.q, rs, :], v).wait_recv)
@@ -485,7 +516,8 @@
         yield from qw
 
     qw = qweights()
-    run(qrest(), chain(0, 92.0), chain(1, 96.5), resid())
+    owns = [own_part(0, 79.0), own_part(1, 85.0)]
+    run(qrest(), weights2(), owns[0], owns[1], chain(0, 92.0), chain(1, 96.0), resid())
     cm.finish()
 
 
@@ -500,7 +532,7 @@
         hb, qb, w2, nq = tb // 2, tb // 4, d // 4, w_qkv.shape[1]
         g = jnp.concatenate([jnp.stack([g1, g2]), jnp.zeros((6, dh), F32)], axis=0)
         bf, f32 = (lambda *v: pltpu.VMEM(v, BF)), (lambda *v: pltpu.VMEM(v, F32))
-        ns = 216
+        ns = 232
         xo, qo = pl.pallas_call(
             block,
             out_shape=[jax.ShapeDtypeStruct((4, 4, 4, tb, dh), BF), jax.ShapeDtypeStruct((4, 16, 2, 2, qb, nq), BF)],
@@ -510,7 +542,8 @@
                 bf(8, tb, dh), f32(8, 8, dh), bf(tb, d), bf(4, 4, tb, d), bf(8, dh, fh), bf(8, dh, fh),
                 bf(ff, d // 2), bf(w_o.shape[0], d // 2), bf(8, dh, nq), bf(tq, w_o.shape[0]),
                 bf(4, tq // 4, fh), bf(4, tq // 4, fh), f32(2, 4, 4, hb, d // 2),
-                f32(2, 4, 4, qb, w2), f32(2, 4, 4, hb, w2), f32(2, 4, qb, w2), f32(2, 4, hb, w2), f32(2, 2, hb, w2),
+                f32(2, 2, 4, 4, qb, w2 // 2), f32(2, 2, 4, 4, hb, w2 // 2), f32(2, 2, 2, 3, hb, w2 // 2),
+                f32(2, 2, 2, hb, w2 // 2),
                 bf(2, hb, d // 2), bf(2, qb, d // 2), bf(2, 2, qb, d // 2), bf(2, 16, qb, nq),
                 bf(4, tb, dh),
                 pltpu.SemaphoreType.DMA((ns,)), pltpu.SemaphoreType.DMA((ns,)), pltpu.SemaphoreType.DMA((28,))],

time: 207 us -> 194 us (0.937)
  Pallas kernels: 197 us -> 183 us
    pallas_call x1, Pallas kernels: 197 us -> 183 us  [body(): pl.pallas_call(block, out_shape=[jax.ShapeDtypeStruct((4, 4, 4, tb, dh),...]
where the time goes in v6:
time: 194 us
  Pallas kernels  183 us (94%)
  local copies, waits for them, and re-layouts  8.82 us (5%)
    pallas_call x1, Pallas kernels, body(): pl.pallas_call(block, out_shape=[jax.ShapeDtypeStruct((4, 4, 4, tb, dh),...  183 us
    unnamed x4, local copies, waits for them, and re-layouts  7.37 us

profile of v6, /device:TPU:1, one launch (start us, length us, event | category | flops | bytes accessed | tf_op | source)
XLA Modules:
  0.0 193.6 jit_solution(5341571436882819677)
XLA Ops:
  0.6 0.1 pad.2.clone
  0.7 0.7 stack.6
  1.4 0.7 stack.7
  2.1 0.7 maximum_maximum_fusion.g
  2.8 183.4 %block.1 = (bf16[4,4,4,64,384]{4,3,2,1,0:T(8,128)(2,1)}, bf16[4,16,2,2,16,768]{5,4,3,2,1,0:T(8,128)(2,1)}) custom-call(bf16[4096,384]{1,0:T(8,128)(2,1)} %x.1, f32[8,384]{1,0:T(8,128)} %maximum_maximum_fusion.g, bf16[384,1536]{1,0:T(8,128)(2,1)} %wg.1, bf16[384,1536]{1,0:T(8,128)(2,1)} %wu.1, bf16[1536,384]{1,0:T(8,128)(2,1)} %wd.1, bf16[4096,256]{1,0:T(8,128)(2,1)} %o.1, ...), custom_call_target="tpu_custom_call" | custom-call | tf_op jit(solution)/shard_map/block/pallas_call | solution.py:536
  186.2 0.0 copy-start
  186.2 4.0 %copy.13 = bf16[4096,384]{1,0:T(8,128)(2,1)} copy(bf16[4096,384]{1,0:T(8,128)(2,1)} %bitcast.3) | data formatting | bytes 6291456
  190.2 0.7 copy-done
  190.9 2.7 %copy.14 = bf16[4096,768]{1,0:T(8,128)(2,1)} copy(bf16[4096,768]{1,0:T(8,128)(2,1)S(1)} %bitcast.2) | data formatting | bytes 12582912
  (1 shorter events, 0.0 us)
Async XLA Ops:
  186.2 4.7 %copy-start = (bf16[4,16,2,2,16,768]{5,4,3,2,1,0:T(8,128)(2,1)S(1)}, bf16[4,16,2,2,16,768]{5,4,3,2,1,0:T(8,128)(2,1)}, u32[]{:S(2)}) copy-start(bf16[4,16,2,2,16,768]{5,4,3,2,1,0:T(8,128)(2,1)} %get-tuple-element.5) | copy-start | bytes 18874372

commit v7 on v6

--- a/solution.py
+++ b/solution.py
@@ -155,7 +155,7 @@
     list(yb)
 
 
-def ring_rs(cm, get, r1p, r1m, fp, fm, res, m, plus, minus, t0, u, lat):
+def ring_rs(cm, get, r1p, r1m, fp, fm, res, m, plus, minus, t0, t1):
     lo, hi, far = (m + 3) % 4, (m + 1) % 4, (m + 2) % 4
     hb = r1p.shape[-2]
     f0, f1 = (Ellipsis, pl.ds(0, hb), slice(None)), (Ellipsis, pl.ds(hb, hb), slice(None))
@@ -163,7 +163,7 @@
     m0 = cm.send(get(far, 1), r1m, minus)
     p1 = cm.send(get(hi, 1), fp.at[f1], plus)
     m1 = cm.send(get(lo, 0), fm.at[f0], minus)
-    yield t0 + 0.5 * u + lat
+    yield t0
     p0.wait_recv()
     v = get(hi, 0)
     v[...] = r1p[...] + v[...]
@@ -172,7 +172,7 @@
     v = get(lo, 1)
     v[...] = r1m[...] + v[...]
     m2 = cm.send(v, fm.at[f1], minus)
-    yield t0 + 1.5 * u + 2.0 * lat
+    yield t1
     p1.wait_recv()
     m1.wait_recv()
     p2.wait_recv()
@@ -296,7 +296,9 @@
             ss = ss + jnp.sum(v * v, axis=-1, keepdims=True)
         r = lax.rsqrt(ss / float(d) + EPS)
         for k in range(8):
-            nb[:, dh * k:dh * (k + 1)] = (xs[k].astype(F32) * r * gb[k, 0:1, :]).astype(BF)
+            for i in range(dh // 128):
+                ls = slice(128 * i, 128 * (i + 1))
+                nb[:, dh * k + 128 * i:dh * k + 128 * (i + 1)] = (xs[k, :, ls].astype(F32) * r * gb[k, i:i + 1, :]).astype(BF)
         part = (pl.ds(0, dc), pl.ds(dc, dc))
         yield from plane_ag(cn, p, lambda k: nb.at[:, part[k]], lambda zi, yi, k: n.at[zi, yi, :, part[k]],
                             lambda v, s: v.at[pl.ds(hb * s, hb), :], 13.0, 6.0, 16.0)
@@ -351,18 +353,18 @@
         p0 = cm.send(wq, blk(m), p.H(2))
         m0 = cm.send(wq, blk(m), p.H(-2))
         qc.append(cm.send(wq, blk(m), p.C))
-        yield 112.0
+        yield 104.0
         p0.wait_recv()
         p1 = cm.send(half(lo, 0), half(lo, 0), p.H(2))
         qc.append(cm.send(blk(lo), blk(lo), p.C))
         m0.wait_recv()
         m1 = cm.send(half(hi, 1), half(hi, 1), p.H(-2))
         qc.append(cm.send(blk(hi), blk(hi), p.C))
-        yield 120.0
+        yield 111.5
         p1.wait_recv()
         m1.wait_recv()
         qc.append(cm.send(blk(far), blk(far), p.C))
-        yield 127.0
+        yield 115.0
         for v in qc:
             v.wait_recv()
 
@@ -385,39 +387,39 @@
             y[s, 2 * zh:2 * zh + 2, :, :, pl.ds(pl.multiple_of(w3 * e + t * tn, tn), tn)] = v.reshape(2, 4, hb, tn)
             return carry
 
-        lax.fori_loop(0, w3 // tn, step, 0)
+        lax.fori_loop(0, w3 // tn, step, 0, unroll=True)
 
     def rr(k):
         return pl.ds(qb * k, qb)
 
     ay, az = (p.y, p.Y(1), p.Y(-1)), (p.z, p.Z(1), p.Z(-1))
 
-    def scatter(s, e, t):
+    def scatter(s, e, t0, t1, t2):
         ca, cb = pl.ds(w3 * e, w4), pl.ds(w3 * e + w4, w4)
 
-        def both(get_a, get_b, r, f, res_a, res_b, ax_a, ax_b, t, u, v):
-            ga = ring_rs(cm, get_a, r.at[s, e, 0], r.at[s, e, 1], f.at[s, e, 0], f.at[s, e, 1], res_a, *ax_a, t, u, v)
-            gb_ = ring_rs(cm, get_b, r.at[s, e, 2], r.at[s, e, 3], f.at[s, e, 2], f.at[s, e, 3], res_b, *ax_b, t, u, v)
+        def both(get_a, get_b, r, f, res_a, res_b, ax_a, ax_b):
+            ga = ring_rs(cm, get_a, r.at[s, e, 0], r.at[s, e, 1], f.at[s, e, 0], f.at[s, e, 1], res_a, *ax_a, t0, t1)
+            gb_ = ring_rs(cm, get_b, r.at[s, e, 2], r.at[s, e, 3], f.at[s, e, 2], f.at[s, e, 3], res_b, *ax_b, t0, t1)
             for q, _ in zip(ga, gb_):
                 yield q
             list(gb_)
 
         yield from both(lambda i, k: y.at[s, :, i, rr(k), ca], lambda i, k: y.at[s, i, :, rr(k), cb], r1, f1,
-                        lambda k: y.at[s, :, p.y, rr(k), ca], lambda k: y.at[s, p.z, :, rr(k), cb], ay, az, t, 3.0, 2.0)
+                        lambda k: y.at[s, :, p.y, rr(k), ca], lambda k: y.at[s, p.z, :, rr(k), cb], ay, az)
         y3, z3 = [p.Y(k) for k in (1, 2, 3)], [p.Z(k) for k in (1, 2, 3)]
-        ga = ring_rs_direct(cm, lambda i: y.at[s, i, p.y, :, ca], r2.at[s, e, 0], s2.at[s, e, 0], p.z, z3, t + 11.0, 4.0)
-        gb_ = ring_rs_direct(cm, lambda i: y.at[s, p.z, i, :, cb], r2.at[s, e, 1], s2.at[s, e, 1], p.y, y3, t + 11.0, 4.0)
+        ga = ring_rs_direct(cm, lambda i: y.at[s, i, p.y, :, ca], r2.at[s, e, 0], s2.at[s, e, 0], p.z, z3, t2, 0.0)
+        gb_ = ring_rs_direct(cm, lambda i: y.at[s, p.z, i, :, cb], r2.at[s, e, 1], s2.at[s, e, 1], p.y, y3, t2, 0.0)
         for q, _ in zip(ga, gb_):
             yield q
         list(gb_)
 
     def weights2():
         for k, (v, sl) in enumerate(down_in):
-            yield (66.0, 75.0, 87.5)[k]
+            yield (66.0, 74.0, 86.3)[k]
             v.wait_recv()
             late.append(cm.send(sl, sl, p.C))
 
-    def own_part(s, t0):
+    def own_part(s, t0, t):
         yield t0 - 2.0
         if s == 0:
             for v in late[:2]:
@@ -426,19 +428,19 @@
         down(2 * s, 0)
         yield t0
         down(2 * s + 1, 0)
-        yield from scatter(s, 0, t0 + 1.0)
-
-    def chain(s, t0):
+        yield from scatter(s, 0, *t)
+
+    def chain(s, t0, dt, t):
         yield t0 - 2.0
         if s == 0:
             for v in late:
                 v.wait_recv()
         down(2 * s, 1)
         down(2 * s + 1, 1)
-        yield from scatter(s, 1, t0 + 1.0)
+        yield from scatter(s, 1, *t)
         for _ in owns[s]:
             pass
-        t = t0 + 18.0
+        t = t0 + 14.5 + dt
         rs = pl.ds(hb * s, hb)
         for e in range(2):
             for k in range(2):
@@ -454,15 +456,18 @@
         oth = xr[s].astype(F32)
         ss = jnp.sum(mine * mine, axis=-1, keepdims=True) + jnp.sum(oth * oth, axis=-1, keepdims=True)
         r = lax.rsqrt(ss / float(d) + EPS)
+        ng = dh // 128
         for k in range(4):
-            cs = slice(dh * k, dh * (k + 1))
-            nh[s, p.j, :, cs] = (mine[:, cs] * r * gb[4 * p.j + k, 1:2, :]).astype(BF)
-            nh[s, 1 - p.j, :, cs] = (oth[:, cs] * r * gb[4 * (1 - p.j) + k, 1:2, :]).astype(BF)
+            for i in range(ng):
+                cs = slice(dh * k + 128 * i, dh * k + 128 * (i + 1))
+                gs = slice(ng + i, ng + i + 1)
+                nh[s, p.j, :, cs] = (mine[:, cs] * r * gb[4 * p.j + k, gs, :]).astype(BF)
+                nh[s, 1 - p.j, :, cs] = (oth[:, cs] * r * gb[4 * (1 - p.j) + k, gs, :]).astype(BF)
         part = (pl.ds(0, dc), pl.ds(dc, dc))
         n1 = n.at[:, :, pl.ds(hb * s, qb), :]
         yield from plane_ag(cm, p, lambda k: nh.at[s, k], lambda zi, yi, k: n1.at[zi, yi, :, part[k]],
                             None, t + 3.0, 3.0, 6.0)
-        yield t + 20.0
+        yield t + 15.5
 
         if s == 0:
             for _ in qw:
@@ -473,7 +478,7 @@
             qk[s, :, :, cs] = _dot(n[:, :, hb * s:hb * s + qb, :].reshape(16 * qb, d), wqb[:, :, cs].reshape(d, tn)).astype(BF).reshape(16, qb, tn)
             return carry
 
-        lax.fori_loop(0, wq.shape[1] // tn, proj, 0)
+        lax.fori_loop(0, wq.shape[1] // tn, proj, 0, unroll=True)
 
         def blk(xx):
             h = 2 * xx + p.c
@@ -487,37 +492,38 @@
         p0 = cm.send(qk.at[s], blk(m), p.H(2))
         m0 = cm.send(qk.at[s], blk(m), p.H(-2))
         c = [cm.send(qk.at[s], blk(m), p.C)]
-        yield t + 31.0
+        yield t + 26.0 + 1.75 * dt
         p0.wait_recv()
         p1 = cm.send(half(lo, 0), half(lo, 0), p.H(2))
         m0.wait_recv()
         m1 = cm.send(half(hi, 1), half(hi, 1), p.H(-2))
         for b in (blk(lo), blk(hi)):
             c.append(cm.send(b, b, p.C))
-        yield t + 38.0
+        yield t + 32.0 + 1.75 * dt
         p1.wait_recv()
         c.append(cm.send(half(far, 0), half(far, 0), p.C))
         m1.wait_recv()
         c.append(cm.send(half(far, 1), half(far, 1), p.C))
-        yield t + 42.0
+        yield t + 35.0 + 1.75 * dt
         own.wait()
         for v in c:
             v.wait_recv()
 
     def resid():
-        yield 134.0
+        yield 130.5
         for wait in xex:
             wait()
         yield from plane_ag(cm, p, lambda k: xq.at[pl.ds(2 * k, 2)], lambda zi, yi, k: x_o.at[pl.ds(2 * k, 2), zi, yi],
-                            None, 134.0, 3.0, 10.0)
+                            None, 131.5, 4.0, 10.0)
 
     def qrest():
+        yield 89.0
         yield next(qw)
         yield from qw
 
     qw = qweights()
-    owns = [own_part(0, 79.0), own_part(1, 85.0)]
-    run(qrest(), weights2(), owns[0], owns[1], chain(0, 92.0), chain(1, 96.0), resid())
+    owns = [own_part(0, 75.0, (81.0, 86.0, 90.0)), own_part(1, 81.0, (87.0, 100.5, 104.0))]
+    run(qrest(), weights2(), owns[0], owns[1], chain(0, 92.0, 0.0, (97.3, 102.3, 106.3)), chain(1, 94.6, 4.0, (99.9, 104.9, 108.9)), resid())
     cm.finish()
 
 
@@ -530,7 +536,7 @@
         tb = tq // 16
         fh = ff // 2
         hb, qb, w2, nq = tb // 2, tb // 4, d // 4, w_qkv.shape[1]
-        g = jnp.concatenate([jnp.stack([g1, g2]), jnp.zeros((6, dh), F32)], axis=0)
+        g = jnp.concatenate([g1, g2]).reshape(2 * dh // 128, 128)
         bf, f32 = (lambda *v: pltpu.VMEM(v, BF)), (lambda *v: pltpu.VMEM(v, F32))
         ns = 232
         xo, qo = pl.pallas_call(
@@ -539,7 +545,7 @@
             in_specs=[HB] * 8,
             out_specs=[ANY] * 2,
             scratch_shapes=[
-                bf(8, tb, dh), f32(8, 8, dh), bf(tb, d), bf(4, 4, tb, d), bf(8, dh, fh), bf(8, dh, fh),
+                bf(8, tb, dh), f32(8, 2 * dh // 128, 128), bf(tb, d), bf(4, 4, tb, d), bf(8, dh, fh), bf(8, dh, fh),
                 bf(ff, d // 2), bf(w_o.shape[0], d // 2), bf(8, dh, nq), bf(tq, w_o.shape[0]),
                 bf(4, tq // 4, fh), bf(4, tq // 4, fh), f32(2, 4, 4, hb, d // 2),
                 f32(2, 2, 4, 4, qb, w2 // 2), f32(2, 2, 4, 4, hb, w2 // 2), f32(2, 2, 2, 3, hb, w2 // 2),

time: 194 us -> 192 us (0.990)
  no operation moved by 1% of the time
where the time goes in v7:
time: 192 us
  Pallas kernels  182 us (95%)
  local copies, waits for them, and re-layouts  7.37 us (4%)
    pallas_call x1, Pallas kernels, body(): pl.pallas_call(block, out_shape=[jax.ShapeDtypeStruct((4, 4, 4, tb, dh),...  182 us
    unnamed x4, local copies, waits for them, and re-layouts  7.37 us

profile of v7, /device:TPU:1, one launch (start us, length us, event | category | flops | bytes accessed | tf_op | source)
XLA Modules:
  0.0 191.6 jit_solution(3268632039589879403)
XLA Ops:
  0.6 1.3 pad_maximum_fusion.g
  1.9 182.3 %block.1 = (bf16[4,4,4,64,384]{4,3,2,1,0:T(8,128)(2,1)}, bf16[4,16,2,2,16,768]{5,4,3,2,1,0:T(8,128)(2,1)}) custom-call(bf16[4096,384]{1,0:T(8,128)(2,1)} %x.1, f32[6,128]{1,0:T(8,128)} %pad_maximum_fusion.g, bf16[384,1536]{1,0:T(8,128)(2,1)} %wg.1, bf16[384,1536]{1,0:T(8,128)(2,1)} %wu.1, bf16[1536,384]{1,0:T(8,128)(2,1)} %wd.1, bf16[4096,256]{1,0:T(8,128)(2,1)} %o.1, ...), custom_call_target="tpu_custom_call" | custom-call | tf_op jit(solution)/shard_map/block/pallas_call | solution.py:542
  184.2 0.0 copy-start
  184.2 4.0 %copy.13 = bf16[4096,384]{1,0:T(8,128)(2,1)} copy(bf16[4096,384]{1,0:T(8,128)(2,1)} %bitcast.5) | data formatting | bytes 6291456
  188.3 0.7 copy-done
  188.9 2.7 %copy.14 = bf16[4096,768]{1,0:T(8,128)(2,1)} copy(bf16[4096,768]{1,0:T(8,128)(2,1)S(1)} %bitcast.4) | data formatting | bytes 12582912
Async XLA Ops:
  184.2 4.7 %copy-start = (bf16[4,16,2,2,16,768]{5,4,3,2,1,0:T(8,128)(2,1)S(1)}, bf16[4,16,2,2,16,768]{5,4,3,2,1,0:T(8,128)(2,1)}, u32[]{:S(2)}) copy-start(bf16[4,16,2,2,16,768]{5,4,3,2,1,0:T(8,128)(2,1)} %get-tuple-element.5) | copy-start | bytes 18874372

commit v8 on v7

--- a/solution.py
+++ b/solution.py
@@ -492,19 +492,19 @@
         p0 = cm.send(qk.at[s], blk(m), p.H(2))
         m0 = cm.send(qk.at[s], blk(m), p.H(-2))
         c = [cm.send(qk.at[s], blk(m), p.C)]
-        yield t + 26.0 + 1.75 * dt
+        yield t + 26.0 - 0.4 * dt
         p0.wait_recv()
         p1 = cm.send(half(lo, 0), half(lo, 0), p.H(2))
         m0.wait_recv()
         m1 = cm.send(half(hi, 1), half(hi, 1), p.H(-2))
         for b in (blk(lo), blk(hi)):
             c.append(cm.send(b, b, p.C))
-        yield t + 32.0 + 1.75 * dt
+        yield t + 32.0 - 0.4 * dt
         p1.wait_recv()
         c.append(cm.send(half(far, 0), half(far, 0), p.C))
         m1.wait_recv()
         c.append(cm.send(half(far, 1), half(far, 1), p.C))
-        yield t + 35.0 + 1.75 * dt
+        yield t + 36.0 + 0.5 * dt
         own.wait()
         for v in c:
             v.wait_recv()
@@ -514,7 +514,7 @@
         for wait in xex:
             wait()
         yield from plane_ag(cm, p, lambda k: xq.at[pl.ds(2 * k, 2)], lambda zi, yi, k: x_o.at[pl.ds(2 * k, 2), zi, yi],
-                            None, 131.5, 4.0, 10.0)
+                            None, 131.5, 4.0, 6.5)
 
     def qrest():
         yield 89.0

time: 192 us -> 189 us (0.984)
  Pallas kernels: 182 us -> 177 us
    pallas_call x1, Pallas kernels: 182 us -> 177 us  [body(): pl.pallas_call(block, out_shape=[jax.ShapeDtypeStruct((4, 4, 4, tb, dh),...]
where the time goes in v8:
time: 189 us; the launch traced here: 187 us
  Pallas kernels  177 us (94%)
  local copies, waits for them, and re-layouts  7.37 us (4%)
    pallas_call x1, Pallas kernels, body(): pl.pallas_call(block, out_shape=[jax.ShapeDtypeStruct((4, 4, 4, tb, dh),...  177 us
    unnamed x4, local copies, waits for them, and re-layouts  7.37 us

profile of v8, /device:TPU:1, one launch (start us, length us, event | category | flops | bytes accessed | tf_op | source)
XLA Modules:
  0.0 186.8 jit_solution(17414707381716175800)
XLA Ops:
  0.6 1.3 pad_maximum_fusion.g
  1.9 177.5 %block.1 = (bf16[4,4,4,64,384]{4,3,2,1,0:T(8,128)(2,1)}, bf16[4,16,2,2,16,768]{5,4,3,2,1,0:T(8,128)(2,1)}) custom-call(bf16[4096,384]{1,0:T(8,128)(2,1)} %x.1, f32[6,128]{1,0:T(8,128)} %pad_maximum_fusion.g, bf16[384,1536]{1,0:T(8,128)(2,1)} %wg.1, bf16[384,1536]{1,0:T(8,128)(2,1)} %wu.1, bf16[1536,384]{1,0:T(8,128)(2,1)} %wd.1, bf16[4096,256]{1,0:T(8,128)(2,1)} %o.1, ...), custom_call_target="tpu_custom_call" | custom-call | tf_op jit(solution)/shard_map/block/pallas_call | solution.py:542
  179.4 0.0 copy-start
  179.4 4.0 %copy.13 = bf16[4096,384]{1,0:T(8,128)(2,1)} copy(bf16[4096,384]{1,0:T(8,128)(2,1)} %bitcast.5) | data formatting | bytes 6291456
  183.4 0.7 copy-done
  184.1 2.7 %copy.14 = bf16[4096,768]{1,0:T(8,128)(2,1)} copy(bf16[4096,768]{1,0:T(8,128)(2,1)S(1)} %bitcast.4) | data formatting | bytes 12582912
Async XLA Ops:
  179.4 4.7 %copy-start = (bf16[4,16,2,2,16,768]{5,4,3,2,1,0:T(8,128)(2,1)S(1)}, bf16[4,16,2,2,16,768]{5,4,3,2,1,0:T(8,128)(2,1)}, u32[]{:S(2)}) copy-start(bf16[4,16,2,2,16,768]{5,4,3,2,1,0:T(8,128)(2,1)} %get-tuple-element.5) | copy-start | bytes 18874372
